TPU v7x, 256 devices: a 4x2x16 block of a 4x16x16 slice. The times are simulated.
256 devices in a mesh: models: 2 (over y), leaf: 128 (over x, z, core).
Axes of the slice: x: 4, y: 2, z: 16, core: 2. Of those that a mesh axis runs over, the one named last changes fastest.
The devices are a block of a 4x16x16 slice.
Arguments:
- slip_rate: float32 [1048576], P(('models', 'leaf')), parts along dimension 0, may hold values from -6 to 6
- near_blocks: bfloat16 [4096, 3, 256, 256], P(('models', 'leaf')), parts along dimension 0, may hold values from -0.21875 to 0.21875
- near_index: int32 [4096, 3], P(('models', 'leaf')), parts along dimension 0, may hold values from 0 to 2047, as said below
- far_left: bfloat16 [11, 32, 1048576], P(None, None, ('models', 'leaf')), parts along dimension 2, may hold values from -1 to 1
- far_right: bfloat16 [11, 32, 1048576], P(None, None, ('models', 'leaf')), parts along dimension 2, may hold values from -6 to 6
- far_ranks: int32 [4096, 11], P(('models', 'leaf')), parts along dimension 0, may hold values from 8 to 32
Outputs:
- first_stress: float32 [1048576], P(('models', 'leaf')), parts along dimension 0
- second_stress: float32 [1048576], P(('models', 'leaf')), parts along dimension 0
There are 2 independent parts, one for each index of `models`. A program takes and returns all parts, laid end to end along the dimension named above; each array names one. Nothing has to cross between parts.
Inputs may be any that keep to these rules, and one draw needn't show every extreme that they name: near_index[i, 0] = i; every other entry is a leaf j != i with |j - i| <= 16, and distance 16 occurs.
All inputs are finite; a program needn't handle non-finite values.
Results may differ from a plain program's by a relative error of at most 0.0045.
Values may be sent and summed in bfloat16 or wider, within the bound.
No kernel may reach another device: no remote copies, remote signals or barrier semaphores. Data moves between devices by JAX's collectives and lax.ppermute only.
A program may use at most 64 MiB of HBM per device.

v0:
```python
import math

import jax
import jax.numpy as jnp
from jax import lax
from jax.sharding import PartitionSpec as P


def partner_2(value, axis, stride):
    return lax.ppermute(value, axis, [(i, i ^ 1 << stride) for i in range(lax.axis_size(axis))])


def padded(block, sides, width):
    for axis, dim in sides:
        count = lax.axis_size(axis)
        forward = [(i, i + 1) for i in range(count - 1)]
        backward = [(target, source) for source, target in forward]
        low = lax.ppermute(
            lax.slice_in_dim(block, block.shape[dim] - width, None, axis=dim), axis, forward
        )
        high = lax.ppermute(lax.slice_in_dim(block, 0, width, axis=dim), axis, backward)
        block = jnp.concatenate([low, block, high], axis=dim)
    return block


def far_partners(device_sums, cross_levels):
    outputs = []
    accumulated = device_sums
    for bit_no in range(cross_levels):
        received = partner_2(accumulated, "leaf", bit_no)
        outputs.append(received[bit_no])
        accumulated = accumulated + received
    return outputs


def matvec(operand, near_blocks, near_index, far_left, far_right, far_ranks):
    local_leaves = near_blocks.shape[0]
    leaf_size = near_blocks.shape[2]
    levels = far_left.shape[0]
    rank_cols = far_left.shape[1]
    slip_rows = operand.reshape(local_leaves, leaf_size)
    extended = padded(slip_rows, (("leaf", 0),), local_leaves)
    offset = lax.axis_index("leaf") * local_leaves - local_leaves
    position = near_index - offset
    onehot = (
        position[:, :, None] == jnp.arange(3 * local_leaves, dtype=jnp.int32)[None, None, :]
    ).astype(jnp.bfloat16)
    picked = jnp.einsum("ikj,jp->ikp", onehot, extended, preferred_element_type=jnp.float32).astype(
        jnp.bfloat16
    )
    result = jnp.einsum("ikpq,ikq->ip", near_blocks, picked, preferred_element_type=jnp.float32)
    right_part = far_right.reshape(levels, rank_cols, local_leaves, leaf_size)
    projected = jnp.einsum(
        "lrcp,cp->lcr", right_part, slip_rows, preferred_element_type=jnp.float32
    )
    local_levels = local_leaves.bit_length() - 1
    cross_levels = levels - local_levels
    columns = []
    for level_no in range(local_levels):
        span_size = 2**level_no
        cluster_sums = (
            projected[level_no].reshape(local_leaves // span_size, span_size, rank_cols).sum(axis=1)
        )
        cluster_sums = cluster_sums * (1.0 / math.sqrt(leaf_size * span_size))
        partner = cluster_sums.reshape(-1, 2, rank_cols)[:, ::-1, :].reshape(-1, rank_cols)
        columns.append(jnp.repeat(partner, span_size, axis=0))
    device_sums = jnp.sum(projected[local_levels:], axis=1)
    partner_list = far_partners(device_sums, cross_levels)
    for bit_no in range(cross_levels):
        scale = 1.0 / math.sqrt(leaf_size * 2 ** (local_levels + bit_no))
        columns.append(
            jnp.broadcast_to(partner_list[bit_no][None, :] * scale, (local_leaves, rank_cols))
        )
    stacked = jnp.stack(columns)
    rank_mask = (
        jnp.arange(rank_cols, dtype=jnp.int32)[None, None, :] < jnp.transpose(far_ranks)[:, :, None]
    )
    weights = jnp.where(rank_mask, stacked, 0.0).astype(jnp.bfloat16)
    left_part = far_left.reshape(levels, rank_cols, local_leaves, leaf_size)
    result = result + jnp.einsum(
        "lrcp,lcr->cp", left_part, weights, preferred_element_type=jnp.float32
    )
    return result.reshape(-1)


def local(slip_rate, near_blocks, near_index, far_left, far_right, far_ranks):
    slip_bf = slip_rate.astype(jnp.bfloat16)
    first_stress = matvec(slip_bf, near_blocks, near_index, far_left, far_right, far_ranks)
    relaxed = slip_rate + jnp.tanh(first_stress / 3.0)
    relaxed_bf = relaxed.astype(jnp.bfloat16)
    second_stress = matvec(relaxed_bf, near_blocks, near_index, far_left, far_right, far_ranks)
    return (first_stress, second_stress)


def solution(mesh):
    in_specs = (
        P(("models", "leaf")),
        P(("models", "leaf"), None, None, None),
        P(("models", "leaf"), None),
        P(None, None, ("models", "leaf")),
        P(None, None, ("models", "leaf")),
        P(("models", "leaf"), None),
    )
    out_specs = (P(("models", "leaf")), P(("models", "leaf")))
    return jax.shard_map(local, mesh=mesh, in_specs=in_specs, out_specs=out_specs, check_vma=False)
```

profile of v0, /device:TPU:40, one launch (start us, length us, event | category | flops | bytes accessed | tf_op | source)
XLA Modules:
  0.0 126.7 jit_solution(1920855411057678525)
XLA Ops:
  2.9 3.1 %collective-permute-start = (bf16[16,256]{1,0:T(8,128)(2,1)S(1)}, bf16[16,256]{1,0:T(8,128)(2,1)S(1)}, u32[]{:S(2)}, u32[]{:S(2)}) collective-permute-start(bf16[16,256]{1,0:T(8,128)(2,1)S(1)} %reshape.104), channel_id=1, source_target_pairs={{0,1},{1,2},{2,3},{3,4},{4,5},{5,6},{6,7},{7,8},{8,9},{9,10},{10,1... | collective-permute-start | bytes 24584 | tf_op jit(solution)/shard_map/ppermute | solution.py:18
  6.0 3.7 %fusion.6 = f32[16,1,11,32]{3,1,2,0:T(1,128)S(1)} fusion(bf16[16,256,1,1]{1,2,3,0:T(2,128)(2,1)S(1)} %reshape.129, bf16[11,4,16,8,256]{4,3,2,1,0:T(8,128)(2,1)} %bitcast.133), kind=kOutput, calls=%fused_computation.6 | convolution fusion | flops 2883584 | bytes 2914304 | tf_op jit(solution)/shard_map/lrcp,cp->lcr/dot_general | solution.py:53
  9.7 2.5 %collective-permute-start.2 = (f32[7,32]{1,0:T(8,128)S(1)}, f32[7,32]{1,0:T(8,128)S(1)}, u32[]{:S(2)}, u32[]{:S(2)}) collective-permute-start(f32[7,32]{1,0:T(8,128)S(1)} %slice_reduce_fusion.1), channel_id=1, source_target_pairs={{0,1},{1,0},{2,3},{3,2},{4,5},{5,4},{6,7},{7,6},{8,9},{9,8},{10,11... | collective-permute-start | bytes 2696 | tf_op jit(solution)/shard_map/ppermute | solution.py:10
  13.0 2.8 %collective-permute-start.3 = (f32[7,32]{1,0:T(8,128)S(1)}, f32[7,32]{1,0:T(8,128)S(1)}, u32[]{:S(2)}, u32[]{:S(2)}) collective-permute-start(f32[7,32]{1,0:T(8,128)S(1)} %add.46), channel_id=1, source_target_pairs={{0,2},{1,3},{2,0},{3,1},{4,6},{5,7},{6,4},{7,5},{8,10},{9,11},{10,... | collective-permute-start | bytes 2696 | tf_op jit(solution)/shard_map/ppermute | solution.py:10
  17.4 6.2 %collective-permute-start.4 = (f32[7,32]{1,0:T(8,128)S(1)}, f32[7,32]{1,0:T(8,128)S(1)}, u32[]{:S(2)}, u32[]{:S(2)}) collective-permute-start(f32[7,32]{1,0:T(8,128)S(1)} %add.47), channel_id=1, source_target_pairs={{0,4},{1,5},{2,6},{3,7},{4,0},{5,1},{6,2},{7,3},{8,12},{9,13},{10,... | collective-permute-start | bytes 2696 | tf_op jit(solution)/shard_map/ppermute | solution.py:10
  23.6 1.6 %collective-permute-done.4 = f32[7,32]{1,0:T(8,128)S(1)} collective-permute-done((f32[7,32]{1,0:T(8,128)S(1)}, f32[7,32]{1,0:T(8,128)S(1)}, u32[]{:S(2)}, u32[]{:S(2)}) %collective-permute-start.4) | collective-permute-done | bytes 928 | tf_op jit(solution)/shard_map/ppermute | solution.py:10
  25.2 10.6 %collective-permute-start.5 = (f32[7,32]{1,0:T(8,128)S(1)}, f32[7,32]{1,0:T(8,128)S(1)}, u32[]{:S(2)}, u32[]{:S(2)}) collective-permute-start(f32[7,32]{1,0:T(8,128)S(1)} %add.48), channel_id=1, source_target_pairs={{0,8},{1,9},{2,10},{3,11},{4,12},{5,13},{6,14},{7,15},{8,0},{9,1},... | collective-permute-start | bytes 2696 | tf_op jit(solution)/shard_map/ppermute | solution.py:10
  35.8 1.6 %collective-permute-done.5 = f32[7,32]{1,0:T(8,128)S(1)} collective-permute-done((f32[7,32]{1,0:T(8,128)S(1)}, f32[7,32]{1,0:T(8,128)S(1)}, u32[]{:S(2)}, u32[]{:S(2)}) %collective-permute-start.5) | collective-permute-done | bytes 928 | tf_op jit(solution)/shard_map/ppermute | solution.py:10
  37.4 12.8 %collective-permute-start.6 = (f32[7,32]{1,0:T(8,128)S(1)}, f32[7,32]{1,0:T(8,128)S(1)}, u32[]{:S(2)}, u32[]{:S(2)}) collective-permute-start(f32[7,32]{1,0:T(8,128)S(1)} %add.49), channel_id=1, source_target_pairs={{0,16},{1,17},{2,18},{3,19},{4,20},{5,21},{6,22},{7,23},{8,24},{9,... | collective-permute-start | bytes 2696 | tf_op jit(solution)/shard_map/ppermute | solution.py:10
  51.8 9.9 %collective-permute-start.7 = (f32[7,32]{1,0:T(8,128)S(1)}, f32[7,32]{1,0:T(8,128)S(1)}, u32[]{:S(2)}, u32[]{:S(2)}) collective-permute-start(f32[7,32]{1,0:T(8,128)S(1)} %add.50), channel_id=1, source_target_pairs={{0,32},{1,33},{2,34},{3,35},{4,36},{5,37},{6,38},{7,39},{8,40},{9,... | collective-permute-start | bytes 2696 | tf_op jit(solution)/shard_map/ppermute | solution.py:10
  63.4 3.7 %collective-permute-start.8 = (f32[7,32]{1,0:T(8,128)S(1)}, f32[7,32]{1,0:T(8,128)S(1)}, u32[]{:S(2)}, u32[]{:S(2)}) collective-permute-start(f32[7,32]{1,0:T(8,128)S(1)} %add.51), channel_id=1, source_target_pairs={{0,64},{1,65},{2,66},{3,67},{4,68},{5,69},{6,70},{7,71},{8,72},{9,... | collective-permute-start | bytes 2696 | tf_op jit(solution)/shard_map/ppermute | solution.py:10
  69.6 4.7 %fusion.16 = f32[16,1,256,1]{2,1,3,0:T(1,128)S(1)} fusion(bf16[16,3,256,256]{3,2,1,0:T(8,128)(2,1)} %param.7, bf16[16,3,256,1]{2,1,0,3:T(4,128)(2,1)S(1)} %bitcast.141), kind=kOutput, calls=%fused_computation.25 | convolution fusion | flops 6291456 | bytes 6332416 | tf_op jit(solution)/shard_map/ikpq,ikq->ip/dot_general | solution.py:51
  75.6 3.1 %collective-permute-start.9 = (bf16[16,256]{1,0:T(8,128)(2,1)S(1)}, bf16[16,256]{1,0:T(8,128)(2,1)S(1)}, u32[]{:S(2)}, u32[]{:S(2)}) collective-permute-start(bf16[16,256]{1,0:T(8,128)(2,1)S(1)} %reshape.110), channel_id=1, source_target_pairs={{0,1},{1,2},{2,3},{3,4},{4,5},{5,6},{6,7},{7,8},{8,9},{9,10},{10,1... | collective-permute-start | bytes 24584 | tf_op jit(solution)/shard_map/ppermute | solution.py:18
  78.7 1.9 %fusion.4 = f32[16,1,11,32]{3,1,2,0:T(1,128)S(1)} fusion(bf16[16,256,1,1]{1,2,3,0:T(2,128)(2,1)S(1)} %reshape.131, bf16[11,4,16,8,256]{4,3,2,1,0:T(8,128)(2,1)S(1)} %bitcast.134), kind=kOutput, calls=%fused_computation.4 | convolution fusion | flops 2883584 | bytes 2914304 | tf_op jit(solution)/shard_map/lrcp,cp->lcr/dot_general | solution.py:53
  82.2 3.5 %collective-permute-done.12 = f32[7,32]{1,0:T(8,128)S(1)} collective-permute-done((f32[7,32]{1,0:T(8,128)S(1)}, f32[7,32]{1,0:T(8,128)S(1)}, u32[]{:S(2)}, u32[]{:S(2)}) %collective-permute-start.12) | collective-permute-done | bytes 928 | tf_op jit(solution)/shard_map/ppermute | solution.py:10
  85.8 4.5 %collective-permute-done.13 = f32[7,32]{1,0:T(8,128)S(1)} collective-permute-done((f32[7,32]{1,0:T(8,128)S(1)}, f32[7,32]{1,0:T(8,128)S(1)}, u32[]{:S(2)}, u32[]{:S(2)}) %collective-permute-start.13) | collective-permute-done | bytes 928 | tf_op jit(solution)/shard_map/ppermute | solution.py:10
  90.3 7.5 %collective-permute-done.14 = f32[7,32]{1,0:T(8,128)S(1)} collective-permute-done((f32[7,32]{1,0:T(8,128)S(1)}, f32[7,32]{1,0:T(8,128)S(1)}, u32[]{:S(2)}, u32[]{:S(2)}) %collective-permute-start.14) | collective-permute-done | bytes 928 | tf_op jit(solution)/shard_map/ppermute | solution.py:10
  97.8 4.1 %collective-permute-start.15 = (f32[7,32]{1,0:T(8,128)S(1)}, f32[7,32]{1,0:T(8,128)S(1)}, u32[]{:S(2)}, u32[]{:S(2)}) collective-permute-start(f32[7,32]{1,0:T(8,128)S(1)} %add.57), channel_id=1, source_target_pairs={{0,16},{1,17},{2,18},{3,19},{4,20},{5,21},{6,22},{7,23},{8,24},{9,... | collective-permute-start | bytes 2696 | tf_op jit(solution)/shard_map/ppermute | solution.py:10
  101.9 8.2 %collective-permute-done.15 = f32[7,32]{1,0:T(8,128)S(1)} collective-permute-done((f32[7,32]{1,0:T(8,128)S(1)}, f32[7,32]{1,0:T(8,128)S(1)}, u32[]{:S(2)}, u32[]{:S(2)}) %collective-permute-start.15) | collective-permute-done | bytes 928 | tf_op jit(solution)/shard_map/ppermute | solution.py:10
  110.1 1.9 %collective-permute-start.16 = (f32[7,32]{1,0:T(8,128)S(1)}, f32[7,32]{1,0:T(8,128)S(1)}, u32[]{:S(2)}, u32[]{:S(2)}) collective-permute-start(f32[7,32]{1,0:T(8,128)S(1)} %add.58), channel_id=1, source_target_pairs={{0,32},{1,33},{2,34},{3,35},{4,36},{5,37},{6,38},{7,39},{8,40},{9,... | collective-permute-start | bytes 2696 | tf_op jit(solution)/shard_map/ppermute | solution.py:10
  112.0 1.7 %collective-permute-done.16 = f32[7,32]{1,0:T(8,128)S(1)} collective-permute-done((f32[7,32]{1,0:T(8,128)S(1)}, f32[7,32]{1,0:T(8,128)S(1)}, u32[]{:S(2)}, u32[]{:S(2)}) %collective-permute-start.16) | collective-permute-done | bytes 928 | tf_op jit(solution)/shard_map/ppermute | solution.py:10
  113.7 3.5 %collective-permute-start.17 = (f32[7,32]{1,0:T(8,128)S(1)}, f32[7,32]{1,0:T(8,128)S(1)}, u32[]{:S(2)}, u32[]{:S(2)}) collective-permute-start(f32[7,32]{1,0:T(8,128)S(1)} %add.59), channel_id=1, source_target_pairs={{0,64},{1,65},{2,66},{3,67},{4,68},{5,69},{6,70},{7,71},{8,72},{9,... | collective-permute-start | bytes 2696 | tf_op jit(solution)/shard_map/ppermute | solution.py:10
  119.0 2.4 %fusion = f32[16,1,256,1]{2,1,3,0:T(1,128)S(1)} fusion(bf16[11,4,16,8,256]{4,3,2,1,0:T(8,128)(2,1)} %bitcast.167, bf16[11,16,32,1]{2,1,0,3:T(8,128)(2,1)S(1)} %fusion.19), kind=kOutput, calls=%fused_computation | convolution fusion | flops 2883584 | bytes 2911232 | tf_op jit(solution)/shard_map/lrcp,lcr->cp/dot_general | solution.py:80
  121.5 4.5 %fusion.14 = f32[16,1,256,1]{2,1,3,0:T(1,128)S(1)} fusion(bf16[16,3,256,256]{3,2,1,0:T(8,128)(2,1)} %param.7, bf16[16,3,256,1]{2,1,0,3:T(4,128)(2,1)S(1)} %bitcast.142), kind=kOutput, calls=%fused_computation.23 | convolution fusion | flops 6291456 | bytes 6332416 | tf_op jit(solution)/shard_map/ikpq,ikq->ip/dot_general | solution.py:51
  (130 shorter events, 15.8 us)
Async XLA Ops:
  0.6 11.6 %copy-start.4 = (s32[16,3]{0,1:T(4,128)S(1)}, s32[16,3]{0,1:T(4,128)}, u32[]{:S(2)}) copy-start(s32[16,3]{0,1:T(4,128)} %param.8) | copy-start | bytes 580
  0.6 12.1 %copy-start.3 = (s32[16,11]{1,0:T(8,128)S(1)}, s32[16,11]{1,0:T(8,128)}, u32[]{:S(2)}) copy-start(s32[16,11]{1,0:T(8,128)} %param.11) | copy-start | bytes 2116
  0.6 68.1 %copy-start.5 = (bf16[11,32,4096]{2,1,0:T(8,128)(2,1)S(1)}, bf16[11,32,4096]{2,1,0:T(8,128)(2,1)}, u32[]{:S(2)}) copy-start(bf16[11,32,4096]{2,1,0:T(8,128)(2,1)} %param.9) | copy-start | bytes 8650756
  1.5 67.8 %collective-permute-start.1 = (bf16[16,256]{1,0:T(8,128)(2,1)S(1)}, bf16[16,256]{1,0:T(8,128)(2,1)S(1)}, u32[]{:S(2)}, u32[]{:S(2)}) collective-permute-start(bf16[16,256]{1,0:T(8,128)(2,1)S(1)} %reshape.104), channel_id=1, source_target_pairs={{1,0},{2,1},{3,2},{4,3},{5,4},{6,5},{7,6},{8,7},{9,8},{10,9},{11,1... | collective-permute-start | bytes 24584 | tf_op jit(solution)/shard_map/ppermute | solution.py:21
  2.9 66.5 %collective-permute-start = (bf16[16,256]{1,0:T(8,128)(2,1)S(1)}, bf16[16,256]{1,0:T(8,128)(2,1)S(1)}, u32[]{:S(2)}, u32[]{:S(2)}) collective-permute-start(bf16[16,256]{1,0:T(8,128)(2,1)S(1)} %reshape.104), channel_id=1, source_target_pairs={{0,1},{1,2},{2,3},{3,4},{4,5},{5,6},{6,7},{7,8},{8,9},{9,10},{10,1... | collective-permute-start | bytes 24584 | tf_op jit(solution)/shard_map/ppermute | solution.py:18
  9.7 3.3 %collective-permute-start.2 = (f32[7,32]{1,0:T(8,128)S(1)}, f32[7,32]{1,0:T(8,128)S(1)}, u32[]{:S(2)}, u32[]{:S(2)}) collective-permute-start(f32[7,32]{1,0:T(8,128)S(1)} %slice_reduce_fusion.1), channel_id=1, source_target_pairs={{0,1},{1,0},{2,3},{3,2},{4,5},{5,4},{6,7},{7,6},{8,9},{9,8},{10,11... | collective-permute-start | bytes 2696 | tf_op jit(solution)/shard_map/ppermute | solution.py:10
  13.0 4.4 %collective-permute-start.3 = (f32[7,32]{1,0:T(8,128)S(1)}, f32[7,32]{1,0:T(8,128)S(1)}, u32[]{:S(2)}, u32[]{:S(2)}) collective-permute-start(f32[7,32]{1,0:T(8,128)S(1)} %add.46), channel_id=1, source_target_pairs={{0,2},{1,3},{2,0},{3,1},{4,6},{5,7},{6,4},{7,5},{8,10},{9,11},{10,... | collective-permute-start | bytes 2696 | tf_op jit(solution)/shard_map/ppermute | solution.py:10
  17.4 7.8 %collective-permute-start.4 = (f32[7,32]{1,0:T(8,128)S(1)}, f32[7,32]{1,0:T(8,128)S(1)}, u32[]{:S(2)}, u32[]{:S(2)}) collective-permute-start(f32[7,32]{1,0:T(8,128)S(1)} %add.47), channel_id=1, source_target_pairs={{0,4},{1,5},{2,6},{3,7},{4,0},{5,1},{6,2},{7,3},{8,12},{9,13},{10,... | collective-permute-start | bytes 2696 | tf_op jit(solution)/shard_map/ppermute | solution.py:10
  25.2 12.2 %collective-permute-start.5 = (f32[7,32]{1,0:T(8,128)S(1)}, f32[7,32]{1,0:T(8,128)S(1)}, u32[]{:S(2)}, u32[]{:S(2)}) collective-permute-start(f32[7,32]{1,0:T(8,128)S(1)} %add.48), channel_id=1, source_target_pairs={{0,8},{1,9},{2,10},{3,11},{4,12},{5,13},{6,14},{7,15},{8,0},{9,1},... | collective-permute-start | bytes 2696 | tf_op jit(solution)/shard_map/ppermute | solution.py:10
  37.4 14.4 %collective-permute-start.6 = (f32[7,32]{1,0:T(8,128)S(1)}, f32[7,32]{1,0:T(8,128)S(1)}, u32[]{:S(2)}, u32[]{:S(2)}) collective-permute-start(f32[7,32]{1,0:T(8,128)S(1)} %add.49), channel_id=1, source_target_pairs={{0,16},{1,17},{2,18},{3,19},{4,20},{5,21},{6,22},{7,23},{8,24},{9,... | collective-permute-start | bytes 2696 | tf_op jit(solution)/shard_map/ppermute | solution.py:10
  51.8 11.5 %collective-permute-start.7 = (f32[7,32]{1,0:T(8,128)S(1)}, f32[7,32]{1,0:T(8,128)S(1)}, u32[]{:S(2)}, u32[]{:S(2)}) collective-permute-start(f32[7,32]{1,0:T(8,128)S(1)} %add.50), channel_id=1, source_target_pairs={{0,32},{1,33},{2,34},{3,35},{4,36},{5,37},{6,38},{7,39},{8,40},{9,... | collective-permute-start | bytes 2696 | tf_op jit(solution)/shard_map/ppermute | solution.py:10
  63.4 5.3 %collective-permute-start.8 = (f32[7,32]{1,0:T(8,128)S(1)}, f32[7,32]{1,0:T(8,128)S(1)}, u32[]{:S(2)}, u32[]{:S(2)}) collective-permute-start(f32[7,32]{1,0:T(8,128)S(1)} %add.51), channel_id=1, source_target_pairs={{0,64},{1,65},{2,66},{3,67},{4,68},{5,69},{6,70},{7,71},{8,72},{9,... | collective-permute-start | bytes 2696 | tf_op jit(solution)/shard_map/ppermute | solution.py:10
  69.5 4.7 %copy-start.1 = (f32[4096]{0:T(1024)S(1)}, f32[4096]{0:T(1024)}, u32[]{:S(2)}) copy-start(f32[4096]{0:T(1024)} %param.6) | copy-start | bytes 49156
  69.5 9.2 %copy-start = (bf16[11,32,4096]{2,1,0:T(8,128)(2,1)S(1)}, bf16[11,32,4096]{2,1,0:T(8,128)(2,1)}, u32[]{:S(2)}) copy-start(bf16[11,32,4096]{2,1,0:T(8,128)(2,1)} %param.10) | copy-start | bytes 8650756
  74.2 47.1 %copy-start.2 = (f32[2,2,8,128]{3,1,2,0:T(2,128)}, f32[2,2,8,128]{3,1,2,0:T(2,128)S(1)}, u32[]{:S(2)}) copy-start(f32[2,2,8,128]{3,1,2,0:T(2,128)S(1)} %copy.35) | copy-start | bytes 49156
  74.3 47.0 %collective-permute-start.10 = (bf16[16,256]{1,0:T(8,128)(2,1)S(1)}, bf16[16,256]{1,0:T(8,128)(2,1)S(1)}, u32[]{:S(2)}, u32[]{:S(2)}) collective-permute-start(bf16[16,256]{1,0:T(8,128)(2,1)S(1)} %reshape.110), channel_id=1, source_target_pairs={{1,0},{2,1},{3,2},{4,3},{5,4},{6,5},{7,6},{8,7},{9,8},{10,9},{11,1... | collective-permute-start | bytes 24584 | tf_op jit(solution)/shard_map/ppermute | solution.py:21
  75.6 45.7 %collective-permute-start.9 = (bf16[16,256]{1,0:T(8,128)(2,1)S(1)}, bf16[16,256]{1,0:T(8,128)(2,1)S(1)}, u32[]{:S(2)}, u32[]{:S(2)}) collective-permute-start(bf16[16,256]{1,0:T(8,128)(2,1)S(1)} %reshape.110), channel_id=1, source_target_pairs={{0,1},{1,2},{2,3},{3,4},{4,5},{5,6},{6,7},{7,8},{8,9},{9,10},{10,1... | collective-permute-start | bytes 24584 | tf_op jit(solution)/shard_map/ppermute | solution.py:18
  80.9 1.3 %collective-permute-start.11 = (f32[7,32]{1,0:T(8,128)S(1)}, f32[7,32]{1,0:T(8,128)S(1)}, u32[]{:S(2)}, u32[]{:S(2)}) collective-permute-start(f32[7,32]{1,0:T(8,128)S(1)} %slice_reduce_fusion), channel_id=1, source_target_pairs={{0,1},{1,0},{2,3},{3,2},{4,5},{5,4},{6,7},{7,6},{8,9},{9,8},{10,11... | collective-permute-start | bytes 2696 | tf_op jit(solution)/shard_map/ppermute | solution.py:10
  82.2 3.6 %collective-permute-start.12 = (f32[7,32]{1,0:T(8,128)S(1)}, f32[7,32]{1,0:T(8,128)S(1)}, u32[]{:S(2)}, u32[]{:S(2)}) collective-permute-start(f32[7,32]{1,0:T(8,128)S(1)} %add.54), channel_id=1, source_target_pairs={{0,2},{1,3},{2,0},{3,1},{4,6},{5,7},{6,4},{7,5},{8,10},{9,11},{10,... | collective-permute-start | bytes 2696 | tf_op jit(solution)/shard_map/ppermute | solution.py:10
  85.8 4.5 %collective-permute-start.13 = (f32[7,32]{1,0:T(8,128)S(1)}, f32[7,32]{1,0:T(8,128)S(1)}, u32[]{:S(2)}, u32[]{:S(2)}) collective-permute-start(f32[7,32]{1,0:T(8,128)S(1)} %add.55), channel_id=1, source_target_pairs={{0,4},{1,5},{2,6},{3,7},{4,0},{5,1},{6,2},{7,3},{8,12},{9,13},{10,... | collective-permute-start | bytes 2696 | tf_op jit(solution)/shard_map/ppermute | solution.py:10
  90.3 7.5 %collective-permute-start.14 = (f32[7,32]{1,0:T(8,128)S(1)}, f32[7,32]{1,0:T(8,128)S(1)}, u32[]{:S(2)}, u32[]{:S(2)}) collective-permute-start(f32[7,32]{1,0:T(8,128)S(1)} %add.56), channel_id=1, source_target_pairs={{0,8},{1,9},{2,10},{3,11},{4,12},{5,13},{6,14},{7,15},{8,0},{9,1},... | collective-permute-start | bytes 2696 | tf_op jit(solution)/shard_map/ppermute | solution.py:10
  97.8 12.3 %collective-permute-start.15 = (f32[7,32]{1,0:T(8,128)S(1)}, f32[7,32]{1,0:T(8,128)S(1)}, u32[]{:S(2)}, u32[]{:S(2)}) collective-permute-start(f32[7,32]{1,0:T(8,128)S(1)} %add.57), channel_id=1, source_target_pairs={{0,16},{1,17},{2,18},{3,19},{4,20},{5,21},{6,22},{7,23},{8,24},{9,... | collective-permute-start | bytes 2696 | tf_op jit(solution)/shard_map/ppermute | solution.py:10
  110.1 3.6 %collective-permute-start.16 = (f32[7,32]{1,0:T(8,128)S(1)}, f32[7,32]{1,0:T(8,128)S(1)}, u32[]{:S(2)}, u32[]{:S(2)}) collective-permute-start(f32[7,32]{1,0:T(8,128)S(1)} %add.58), channel_id=1, source_target_pairs={{0,32},{1,33},{2,34},{3,35},{4,36},{5,37},{6,38},{7,39},{8,40},{9,... | collective-permute-start | bytes 2696 | tf_op jit(solution)/shard_map/ppermute | solution.py:10
  113.7 5.1 %collective-permute-start.17 = (f32[7,32]{1,0:T(8,128)S(1)}, f32[7,32]{1,0:T(8,128)S(1)}, u32[]{:S(2)}, u32[]{:S(2)}) collective-permute-start(f32[7,32]{1,0:T(8,128)S(1)} %add.59), channel_id=1, source_target_pairs={{0,64},{1,65},{2,66},{3,67},{4,68},{5,69},{6,70},{7,71},{8,72},{9,... | collective-permute-start | bytes 2696 | tf_op jit(solution)/shard_map/ppermute | solution.py:10
where the time goes:
time: 127 us
  starting transfers between devices  67 us (53%)
  waiting for transfers between devices  37.7 us (30%)
  matrix products  17.9 us (14%)
  other arithmetic  1.49 us (1%)
  local copies, waits for them, and re-layouts  1.47 us (1%)
    ppermute x14, starting transfers between devices, partner_2(): lax.ppermute(value, axis, [(i, i ^ 1 << stride) for i in range(lax.axis_s...  58.3 us
    ppermute x14, waiting for transfers between devices, partner_2(): lax.ppermute(value, axis, [(i, i ^ 1 << stride) for i in range(lax.axis_s...  37.7 us
    dot_general x2, matrix products, matvec(): jnp.einsum('ikpq,ikq->ip', near_blocks, picked, preferred_element_type=jn...  9.15 us
    ppermute x2, starting transfers between devices, padded(): lax.ppermute(lax.slice_in_dim(block, block.shape[dim] - width, None, axis...  6.15 us
    dot_general x2, matrix products, matvec(): jnp.einsum('lrcp,cp->lcr', right_part, slip_rows, preferred_element_type=...  5.54 us
    dot_general x2, matrix products, matvec(): jnp.einsum('lrcp,lcr->cp', left_part, weights, preferred_element_type=jnp...  2.95 us
    ppermute x2, starting transfers between devices, padded(): lax.ppermute(lax.slice_in_dim(block, 0, width, axis=dim), axis, backward)  2.61 us
  transfers between devices with their start and end apart: 18, of which 14 were waited for; matrix products, arithmetic and copies ran while one was open for 8% of the time, Pallas kernels for 0%

commit v1 on v0

--- a/solution.py
+++ b/solution.py
@@ -24,12 +24,22 @@
 
 
 def far_partners(device_sums, cross_levels):
-    outputs = []
-    accumulated = device_sums
-    for bit_no in range(cross_levels):
-        received = partner_2(accumulated, "leaf", bit_no)
-        outputs.append(received[bit_no])
-        accumulated = accumulated + received
+    count = lax.axis_size("leaf")
+    received = partner_2(device_sums, "leaf", 0)
+    chip_sums = device_sums + received
+    chips = count // 2
+    me = lax.axis_index("leaf") // 2
+    apart = jnp.arange(chips, dtype=jnp.int32) ^ me
+    masks = [(apart >> bit_no) == 1 for bit_no in range(cross_levels - 1)]
+    outgoing = sum(
+        jnp.where(mask[:, None], chip_sums[bit_no + 1][None, :], 0.0)
+        for bit_no, mask in enumerate(masks)
+    )
+    groups = [[chip * 2 + core for chip in range(chips)] for core in range(2)]
+    incoming = lax.all_to_all(outgoing, "leaf", 0, 0, axis_index_groups=groups, tiled=True)
+    outputs = [received[0]]
+    for mask in masks:
+        outputs.append(jnp.sum(jnp.where(mask[:, None], incoming, 0.0), axis=0))
     return outputs
 
 

time: 127 us -> 93.1 us (0.73)
  waiting for transfers between devices: 37.7 us -> 18.2 us
  starting transfers between devices: 67 us -> 50.1 us
  other arithmetic: 1.49 us -> 3.93 us
    ppermute x14 -> x2, starting transfers between devices: 58.3 us -> 2.86 us  [partner_2(): lax.ppermute(value, axis, [(i, i ^ 1 << stride) for i in range(lax.axis_s...]
    all_to_all x0 -> x2, starting transfers between devices: none -> 38.5 us  [far_partners(): lax.all_to_all(outgoing, 'leaf', 0, 0, axis_index_groups=groups, tiled=True)]
    ppermute x14 -> x2, waiting for transfers between devices: 37.7 us -> 1.28 us  [partner_2(): lax.ppermute(value, axis, [(i, i ^ 1 << stride) for i in range(lax.axis_s...]
    all_to_all x0 -> x2, waiting for transfers between devices: none -> 16.9 us  [far_partners(): lax.all_to_all(outgoing, 'leaf', 0, 0, axis_index_groups=groups, tiled=True)]
    add x12 -> x4, other arithmetic: 0.04 us -> 2.42 us  [the longest x2 2.42 us: far_partners(): sum((jnp.where(mask[:, None], chip_sums[bit_no + 1][None, :], 0.0) for bi...]
  transfers between devices with their start and end apart: 18 -> 8, of which waited for: 14 -> 4; matrix products, arithmetic and copies ran while one was open for 8% -> 20% of each run, Pallas kernels for 0% -> 0%
where the time goes in v1:
time: 93.1 us; the launch traced here: 92.6 us
  starting transfers between devices  50.1 us (54%)
  waiting for transfers between devices  18.2 us (20%)
  matrix products  18 us (19%)
  other arithmetic  3.93 us (4%)
  local copies, waits for them, and re-layouts  1.3 us (1%)
  between operations  1.09 us (1%)
    all_to_all x2, starting transfers between devices, far_partners(): lax.all_to_all(outgoing, 'leaf', 0, 0, axis_index_groups=groups, tiled=True)  38.5 us
    all_to_all x2, waiting for transfers between devices, far_partners(): lax.all_to_all(outgoing, 'leaf', 0, 0, axis_index_groups=groups, tiled=True)  16.9 us
    dot_general x2, matrix products, matvec(): jnp.einsum('ikpq,ikq->ip', near_blocks, picked, preferred_element_type=jn...  9.15 us
    ppermute x2, starting transfers between devices, padded(): lax.ppermute(lax.slice_in_dim(block, block.shape[dim] - width, None, axis...  6.15 us
    dot_general x2, matrix products, matvec(): jnp.einsum('lrcp,cp->lcr', right_part, slip_rows, preferred_element_type=...  5.54 us
    dot_general x2, matrix products, matvec(): jnp.einsum('lrcp,lcr->cp', left_part, weights, preferred_element_type=jnp...  2.95 us
    ppermute x2, starting transfers between devices, partner_2(): lax.ppermute(value, axis, [(i, i ^ 1 << stride) for i in range(lax.axis_s...  2.86 us
    ppermute x2, starting transfers between devices, padded(): lax.ppermute(lax.slice_in_dim(block, 0, width, axis=dim), axis, backward)  2.61 us
  transfers between devices with their start and end apart: 8, of which 4 were waited for; matrix products, arithmetic and copies ran while one was open for 20% of the time, Pallas kernels for 0%

profile of v1, /device:TPU:40, one launch (start us, length us, event | category | flops | bytes accessed | tf_op | source)
XLA Modules:
  0.0 92.6 jit_solution(16691616974397832777)
XLA Ops:
  0.6 0.7 convert_element_type.20
  1.4 1.3 %collective-permute-start.1 = (bf16[16,256]{1,0:T(8,128)(2,1)S(1)}, bf16[16,256]{1,0:T(8,128)(2,1)S(1)}, u32[]{:S(2)}, u32[]{:S(2)}) collective-permute-start(bf16[16,256]{1,0:T(8,128)(2,1)S(1)} %reshape.752), channel_id=1, source_target_pairs={{1,0},{2,1},{3,2},{4,3},{5,4},{6,5},{7,6},{8,7},{9,8},{10,9},{11,1... | collective-permute-start | bytes 24584 | tf_op jit(solution)/shard_map/ppermute | solution.py:21
  2.7 3.1 %collective-permute-start = (bf16[16,256]{1,0:T(8,128)(2,1)S(1)}, bf16[16,256]{1,0:T(8,128)(2,1)S(1)}, u32[]{:S(2)}, u32[]{:S(2)}) collective-permute-start(bf16[16,256]{1,0:T(8,128)(2,1)S(1)} %reshape.752), channel_id=1, source_target_pairs={{0,1},{1,2},{2,3},{3,4},{4,5},{5,6},{6,7},{7,8},{8,9},{9,10},{10,1... | collective-permute-start | bytes 24584 | tf_op jit(solution)/shard_map/ppermute | solution.py:18
  5.8 3.7 %fusion.6 = f32[16,1,11,32]{3,1,2,0:T(1,128)S(1)} fusion(bf16[16,256,1,1]{1,2,3,0:T(2,128)(2,1)S(1)} %reshape.777, bf16[11,4,16,8,256]{4,3,2,1,0:T(8,128)(2,1)} %bitcast.133), kind=kOutput, calls=%fused_computation.6 | convolution fusion | flops 2883584 | bytes 2914304 | tf_op jit(solution)/shard_map/lrcp,cp->lcr/dot_general | solution.py:63
  9.5 2.5 %collective-permute-start.2 = (f32[7,32]{1,0:T(8,128)S(1)}, f32[7,32]{1,0:T(8,128)S(1)}, u32[]{:S(2)}, u32[]{:S(2)}) collective-permute-start(f32[7,32]{1,0:T(8,128)S(1)} %slice_reduce_fusion.1), channel_id=1, source_target_pairs={{0,1},{1,0},{2,3},{3,2},{4,5},{5,4},{6,7},{7,6},{8,9},{9,8},{10,11... | collective-permute-start | bytes 2696 | tf_op jit(solution)/shard_map/ppermute | solution.py:10
  12.5 0.4 collective-permute-done.2
  12.9 1.2 %fusion.30 = f32[64,1,32]{2,1,0:T(1,128)} fusion(pred[64]{0:T(512)(128)(4,1)S(1)} %get-tuple-element.32, pred[64]{0:T(512)(128)(4,1)S(1)} %get-tuple-element.33, pred[64]{0:T(512)(128)(4,1)S(1)} %get-tuple-element.34, pred[64]{0:T(512)(128)(4,1)S(1)} %get-tuple-element.35, pred[64]{0:T(512)(128)(4,1)S(1)} %get-tuple-element.36, ...), kind=kLoop, calls=%fused_computation.73 | loop fusion | flops 22528 | bytes 9344 | tf_op jit(solution)/shard_map/add | solution.py:34
  14.1 29.9 %all-to-all-start = ((f32[64,1,32]{2,1,0:T(1,128)}), f32[64,1,32]{2,1,0:T(1,128)S(1)}, u32[]{:S(2)}, u32[]{:S(2)}) async-start(f32[64,1,32]{2,1,0:T(1,128)} %fusion.30), calls=%async_computation | async-start | bytes 65536 | tf_op jit(solution)/shard_map/all_to_all | solution.py:39
  44.0 0.2 fusion.12
  44.2 4.5 %fusion.18 = f32[16,1,256,1]{2,1,3,0:T(1,128)S(1)} fusion(bf16[16,3,256,256]{3,2,1,0:T(8,128)(2,1)} %param.7, bf16[16,3,256,1]{2,0,1,3:T(8,128)(2,1)S(1)} %fusion.12), kind=kOutput, calls=%fused_computation.39 | convolution fusion | flops 6291456 | bytes 6332416 | tf_op jit(solution)/shard_map/ikpq,ikq->ip/dot_general | solution.py:61
  48.7 8.5 %all-to-all-done = f32[64,1,32]{2,1,0:T(1,128)S(1)} async-done(((f32[64,1,32]{2,1,0:T(1,128)}), f32[64,1,32]{2,1,0:T(1,128)S(1)}, u32[]{:S(2)}, u32[]{:S(2)}) %all-to-all-start) | async-done | bytes 8224 | tf_op jit(solution)/shard_map/all_to_all | solution.py:39
  57.6 2.4 %fusion.2 = f32[16,1,256,1]{2,1,3,0:T(1,128)S(1)} fusion(bf16[11,4,16,8,256]{4,3,2,1,0:T(8,128)(2,1)} %bitcast.167, bf16[11,16,32,1]{2,1,0,3:T(8,128)(2,1)S(1)} %fusion.20), kind=kOutput, calls=%fused_computation.2 | convolution fusion | flops 2883584 | bytes 2911232 | tf_op jit(solution)/shard_map/lrcp,lcr->cp/dot_general | solution.py:90
  60.1 1.3 %collective-permute-start.4 = (bf16[16,256]{1,0:T(8,128)(2,1)S(1)}, bf16[16,256]{1,0:T(8,128)(2,1)S(1)}, u32[]{:S(2)}, u32[]{:S(2)}) collective-permute-start(bf16[16,256]{1,0:T(8,128)(2,1)S(1)} %reshape.758), channel_id=1, source_target_pairs={{1,0},{2,1},{3,2},{4,3},{5,4},{6,5},{7,6},{8,7},{9,8},{10,9},{11,1... | collective-permute-start | bytes 24584 | tf_op jit(solution)/shard_map/ppermute | solution.py:21
  61.4 3.1 %collective-permute-start.3 = (bf16[16,256]{1,0:T(8,128)(2,1)S(1)}, bf16[16,256]{1,0:T(8,128)(2,1)S(1)}, u32[]{:S(2)}, u32[]{:S(2)}) collective-permute-start(bf16[16,256]{1,0:T(8,128)(2,1)S(1)} %reshape.758), channel_id=1, source_target_pairs={{0,1},{1,2},{2,3},{3,4},{4,5},{5,6},{6,7},{7,8},{8,9},{9,10},{10,1... | collective-permute-start | bytes 24584 | tf_op jit(solution)/shard_map/ppermute | solution.py:18
  64.5 1.9 %fusion.4 = f32[16,1,11,32]{3,1,2,0:T(1,128)S(1)} fusion(bf16[16,256,1,1]{1,2,3,0:T(2,128)(2,1)S(1)} %reshape.779, bf16[11,4,16,8,256]{4,3,2,1,0:T(8,128)(2,1)S(1)} %bitcast.134), kind=kOutput, calls=%fused_computation.4 | convolution fusion | flops 2883584 | bytes 2914304 | tf_op jit(solution)/shard_map/lrcp,cp->lcr/dot_general | solution.py:63
  66.7 0.3 collective-permute-start.5
  67.0 0.9 collective-permute-done.5
  68.0 1.2 %fusion.31 = f32[64,1,32]{2,1,0:T(1,128)} fusion(pred[64]{0:T(512)(128)(4,1)S(1)} %get-tuple-element.32, pred[64]{0:T(512)(128)(4,1)S(1)} %get-tuple-element.33, pred[64]{0:T(512)(128)(4,1)S(1)} %get-tuple-element.34, pred[64]{0:T(512)(128)(4,1)S(1)} %get-tuple-element.35, pred[64]{0:T(512)(128)(4,1)S(1)} %get-tuple-element.36, ...), kind=kLoop, calls=%fused_computation.74 | loop fusion | flops 22528 | bytes 9344 | tf_op jit(solution)/shard_map/add | solution.py:34
  69.2 8.6 %all-to-all-start.1 = ((f32[64,1,32]{2,1,0:T(1,128)}), f32[64,1,32]{2,1,0:T(1,128)S(1)}, u32[]{:S(2)}, u32[]{:S(2)}) async-start(f32[64,1,32]{2,1,0:T(1,128)} %fusion.31), calls=%async_computation.1 | async-start | bytes 65536 | tf_op jit(solution)/shard_map/all_to_all | solution.py:39
  77.8 0.2 fusion.13
  78.0 4.7 %fusion.16 = f32[16,1,256,1]{2,1,3,0:T(1,128)S(1)} fusion(bf16[16,3,256,256]{3,2,1,0:T(8,128)(2,1)} %param.7, bf16[16,3,256,1]{2,0,1,3:T(8,128)(2,1)S(1)} %fusion.13), kind=kOutput, calls=%fused_computation.37 | convolution fusion | flops 6291456 | bytes 6332416 | tf_op jit(solution)/shard_map/ikpq,ikq->ip/dot_general | solution.py:61
  82.7 8.4 %all-to-all-done.1 = f32[64,1,32]{2,1,0:T(1,128)S(1)} async-done(((f32[64,1,32]{2,1,0:T(1,128)}), f32[64,1,32]{2,1,0:T(1,128)S(1)}, u32[]{:S(2)}, u32[]{:S(2)}) %all-to-all-start.1) | async-done | bytes 8224 | tf_op jit(solution)/shard_map/all_to_all | solution.py:39
  91.4 0.6 fusion
  92.0 0.6 copy.34
  (105 shorter events, 1.5 us)
Async XLA Ops:
  0.6 11.7 %copy-start.4 = (s32[16,3]{0,1:T(4,128)S(1)}, s32[16,3]{0,1:T(4,128)}, u32[]{:S(2)}) copy-start(s32[16,3]{0,1:T(4,128)} %param.8) | copy-start | bytes 580
  0.6 11.8 %copy-start.3 = (s32[16,11]{1,0:T(8,128)S(1)}, s32[16,11]{1,0:T(8,128)}, u32[]{:S(2)}) copy-start(s32[16,11]{1,0:T(8,128)} %param.11) | copy-start | bytes 2116
  1.4 42.6 %collective-permute-start.1 = (bf16[16,256]{1,0:T(8,128)(2,1)S(1)}, bf16[16,256]{1,0:T(8,128)(2,1)S(1)}, u32[]{:S(2)}, u32[]{:S(2)}) collective-permute-start(bf16[16,256]{1,0:T(8,128)(2,1)S(1)} %reshape.752), channel_id=1, source_target_pairs={{1,0},{2,1},{3,2},{4,3},{5,4},{6,5},{7,6},{8,7},{9,8},{10,9},{11,1... | collective-permute-start | bytes 24584 | tf_op jit(solution)/shard_map/ppermute | solution.py:21
  2.7 41.3 %collective-permute-start = (bf16[16,256]{1,0:T(8,128)(2,1)S(1)}, bf16[16,256]{1,0:T(8,128)(2,1)S(1)}, u32[]{:S(2)}, u32[]{:S(2)}) collective-permute-start(bf16[16,256]{1,0:T(8,128)(2,1)S(1)} %reshape.752), channel_id=1, source_target_pairs={{0,1},{1,2},{2,3},{3,4},{4,5},{5,6},{6,7},{7,8},{8,9},{9,10},{10,1... | collective-permute-start | bytes 24584 | tf_op jit(solution)/shard_map/ppermute | solution.py:18
  9.5 3.3 %collective-permute-start.2 = (f32[7,32]{1,0:T(8,128)S(1)}, f32[7,32]{1,0:T(8,128)S(1)}, u32[]{:S(2)}, u32[]{:S(2)}) collective-permute-start(f32[7,32]{1,0:T(8,128)S(1)} %slice_reduce_fusion.1), channel_id=1, source_target_pairs={{0,1},{1,0},{2,3},{3,2},{4,5},{5,4},{6,7},{7,6},{8,9},{9,8},{10,11... | collective-permute-start | bytes 2696 | tf_op jit(solution)/shard_map/ppermute | solution.py:10
  14.1 43.2 %all-to-all-start = ((f32[64,1,32]{2,1,0:T(1,128)}), f32[64,1,32]{2,1,0:T(1,128)S(1)}, u32[]{:S(2)}, u32[]{:S(2)}) async-start(f32[64,1,32]{2,1,0:T(1,128)} %fusion.30), calls=%async_computation | async-start | bytes 65536 | tf_op jit(solution)/shard_map/all_to_all | solution.py:39
  48.7 11.3 %copy-start.1 = (f32[4096]{0:T(1024)S(1)}, f32[4096]{0:T(1024)}, u32[]{:S(2)}) copy-start(f32[4096]{0:T(1024)} %param.6) | copy-start | bytes 49156
  48.7 15.8 %copy-start = (bf16[11,32,4096]{2,1,0:T(8,128)(2,1)S(1)}, bf16[11,32,4096]{2,1,0:T(8,128)(2,1)}, u32[]{:S(2)}) copy-start(bf16[11,32,4096]{2,1,0:T(8,128)(2,1)} %param.10) | copy-start | bytes 8650756
  60.0 22.6 %copy-start.2 = (f32[2,2,8,128]{3,1,2,0:T(2,128)}, f32[2,2,8,128]{3,1,2,0:T(2,128)S(1)}, u32[]{:S(2)}) copy-start(f32[2,2,8,128]{3,1,2,0:T(2,128)S(1)} %copy.33) | copy-start | bytes 49156
  60.1 17.7 %collective-permute-start.4 = (bf16[16,256]{1,0:T(8,128)(2,1)S(1)}, bf16[16,256]{1,0:T(8,128)(2,1)S(1)}, u32[]{:S(2)}, u32[]{:S(2)}) collective-permute-start(bf16[16,256]{1,0:T(8,128)(2,1)S(1)} %reshape.758), channel_id=1, source_target_pairs={{1,0},{2,1},{3,2},{4,3},{5,4},{6,5},{7,6},{8,7},{9,8},{10,9},{11,1... | collective-permute-start | bytes 24584 | tf_op jit(solution)/shard_map/ppermute | solution.py:21
  61.4 16.4 %collective-permute-start.3 = (bf16[16,256]{1,0:T(8,128)(2,1)S(1)}, bf16[16,256]{1,0:T(8,128)(2,1)S(1)}, u32[]{:S(2)}, u32[]{:S(2)}) collective-permute-start(bf16[16,256]{1,0:T(8,128)(2,1)S(1)} %reshape.758), channel_id=1, source_target_pairs={{0,1},{1,2},{2,3},{3,4},{4,5},{5,6},{6,7},{7,8},{8,9},{9,10},{10,1... | collective-permute-start | bytes 24584 | tf_op jit(solution)/shard_map/ppermute | solution.py:18
  66.7 1.3 %collective-permute-start.5 = (f32[7,32]{1,0:T(8,128)S(1)}, f32[7,32]{1,0:T(8,128)S(1)}, u32[]{:S(2)}, u32[]{:S(2)}) collective-permute-start(f32[7,32]{1,0:T(8,128)S(1)} %slice_reduce_fusion), channel_id=1, source_target_pairs={{0,1},{1,0},{2,3},{3,2},{4,5},{5,4},{6,7},{7,6},{8,9},{9,8},{10,11... | collective-permute-start | bytes 2696 | tf_op jit(solution)/shard_map/ppermute | solution.py:10
  69.2 21.9 %all-to-all-start.1 = ((f32[64,1,32]{2,1,0:T(1,128)}), f32[64,1,32]{2,1,0:T(1,128)S(1)}, u32[]{:S(2)}, u32[]{:S(2)}) async-start(f32[64,1,32]{2,1,0:T(1,128)} %fusion.31), calls=%async_computation.1 | async-start | bytes 65536 | tf_op jit(solution)/shard_map/all_to_all | solution.py:39
  78.0 13.4 %copy-start.5 = (bf16[11,32,4096]{2,1,0:T(8,128)(2,1)S(1)}, bf16[11,32,4096]{2,1,0:T(8,128)(2,1)}, u32[]{:S(2)}) copy-start(bf16[11,32,4096]{2,1,0:T(8,128)(2,1)} %param.9) | copy-start | bytes 8650756

commit v2 on v0

v2 whole, which is shorter than its diff:
```python
import math

import jax
import jax.numpy as jnp
from jax import lax
from jax.experimental import pallas as pl
from jax.experimental.pallas import tpu as pltpu
from jax.sharding import PartitionSpec as P


F32 = jnp.float32
BF16 = jnp.bfloat16
LANES = 128
NT = (((1,), (1,)), ((), ()))
VMEM_SPEC = pl.BlockSpec(memory_space=pltpu.VMEM)
ANY_SPEC = pl.BlockSpec(memory_space=pl.ANY)


def params(mib):
    return pltpu.CompilerParams(vmem_limit_bytes=mib << 20)


def sums_row(total):
    pad = -total.shape[1] % LANES
    return jnp.concatenate([total, jnp.zeros((1, pad), F32)], axis=1) if pad else total


def leaf_rows(flat):
    leaves = flat.shape[0] // 2
    return jnp.concatenate([flat[pl.ds(0, leaves, stride=2), :], flat[pl.ds(1, leaves, stride=2), :]], axis=1)


def put_rows(flat, rows):
    leaves = rows.shape[0]
    flat[pl.ds(0, leaves, stride=2), :] = rows[:, :LANES]
    flat[pl.ds(1, leaves, stride=2), :] = rows[:, LANES:]


def project_kernel(sizes, slip_hbm, far_right, sums, halo, slip, right_cross, sems):
    leaves, leaf_size, steps = sizes["leaves"], sizes["leaf_size"], sizes["steps"]
    width = leaves // steps * leaf_size
    cross = pl.ds(sizes["cross_row"], sizes["rows"] - sizes["cross_row"])
    copies = [pltpu.make_async_copy(slip_hbm, slip, sems.at[steps])]
    for c in range(steps):
        columns = pl.ds(c * width, width)
        copies.append(pltpu.make_async_copy(far_right.at[cross, columns], right_cross.at[:, columns], sems.at[c]))
    for copy in copies:
        copy.start()
    copies[0].wait()
    rows = leaf_rows(slip).astype(BF16)
    halo[...] = rows
    total = jnp.zeros((1, right_cross.shape[0]), F32)
    for leaf in range(leaves):
        if leaf % (leaves // steps) == 0:
            copies[1 + leaf // (leaves // steps)].wait()
        columns = slice(leaf * leaf_size, (leaf + 1) * leaf_size)
        total += lax.dot_general(rows[leaf : leaf + 1, :], right_cross[:, columns], NT, preferred_element_type=F32)
    sums[...] = sums_row(total)


def siblings(chip, bit_no):
    return (chip >> bit_no ^ 1) << bit_no


def spread_kernel(sizes, own, received, outgoing):
    chip = lax.axis_index("leaf") // 2
    total = own[...] + received[...]
    last = outgoing.shape[0] - 1
    outgoing[last - chip] = total[:, 0:LANES]
    for bit_no in range(sizes["cross_levels"] - 1):
        tile = sizes["rank"] * (bit_no + 1) // LANES * LANES
        start = siblings(chip, bit_no)
        for step in range(2**bit_no):
            outgoing[last - start - step] = total[:, tile : tile + LANES]


def near_part(sizes, index_copy, ranks, own, swap, cross, blocks, right, left, near_index, extended, total):
    leaves, leaf_size, near = sizes["leaves"], sizes["leaf_size"], sizes["near"]
    local_levels, rank = sizes["local_levels"], sizes["rank"]
    local_rows = local_levels * rank
    device = lax.axis_index("leaf")
    odd = device % 2
    extended[pl.ds(leaves, leaves), :] = own[...].astype(F32)
    extended[pl.ds((1 - odd) * 2 * leaves, leaves), :] = swap[...].astype(F32)
    extended[pl.ds(odd * 2 * leaves, leaves), :] = cross[...].astype(F32)
    mine = own[...]
    projected = jnp.concatenate(
        [
            lax.dot_general(
                mine[leaf : leaf + 1, :],
                right[:local_rows, leaf * leaf_size : (leaf + 1) * leaf_size],
                NT,
                preferred_element_type=F32,
            )
            for leaf in range(leaves)
        ],
        axis=0,
    )
    row = lax.broadcasted_iota(jnp.int32, projected.shape, 0)
    lane = lax.broadcasted_iota(jnp.int32, projected.shape, 1)
    level_of = lane // rank
    stacked = jnp.zeros_like(projected)
    limit = jnp.zeros_like(row)
    sums = projected
    for level_no in range(local_levels):
        span = 2**level_no
        partner = jnp.where(
            row // span % 2 == 0,
            pltpu.roll(sums, leaves - span, 0),
            pltpu.roll(sums, span, 0),
        )
        stacked = jnp.where(level_of == level_no, partner * (1.0 / math.sqrt(leaf_size * span)), stacked)
        limit = jnp.where(level_of == level_no, ranks[:, level_no : level_no + 1], limit)
        sums = sums + partner
    weights = jnp.where(lane % rank < limit, stacked, 0.0).astype(BF16)
    for leaf in range(leaves):
        columns = slice(leaf * leaf_size, (leaf + 1) * leaf_size)
        far = jnp.dot(weights, left[:local_rows, columns], preferred_element_type=F32)
        row = lax.dot_general(mine[leaf : leaf + 1, :], blocks[leaf, 0], NT, preferred_element_type=F32)
        total[leaf : leaf + 1, :] = row + far[leaf : leaf + 1, :]
    index_copy.wait()
    base = (device - 1) * leaves
    for leaf in range(leaves):
        row = total[leaf : leaf + 1, :]
        for k in range(1, near):
            picked = extended[pl.ds(near_index[k, leaf] - base, 1), :].astype(BF16)
            row += lax.dot_general(picked, blocks[leaf, k], NT, preferred_element_type=F32)
        total[leaf : leaf + 1, :] = row


def cross_weights(sizes, ranks, swapped, incoming):
    rank, leaf_size, leaves = sizes["rank"], sizes["leaf_size"], sizes["leaves"]
    local_levels, cross_levels = sizes["local_levels"], sizes["cross_levels"]
    chip = lax.axis_index("leaf") // 2
    sums = swapped[...] * (1.0 / math.sqrt(leaf_size * 2**local_levels))
    bit_of = lax.broadcasted_iota(jnp.int32, sums.shape, 1) // rank
    for bit_no in range(cross_levels - 1):
        start = siblings(chip, bit_no)
        start = incoming.shape[0] - 1 - start
        total = incoming[start]
        for step in range(1, 2**bit_no):
            total += incoming[start - step]
        total = jnp.concatenate([total] * (sums.shape[1] // LANES), axis=1)
        scale = 1.0 / math.sqrt(leaf_size * 2 ** (local_levels + 1 + bit_no))
        sums = jnp.where(bit_of == 1 + bit_no, total * scale, sums)
    width = cross_levels * rank
    lane = lax.broadcasted_iota(jnp.int32, (leaves, width), 1)
    limit = jnp.zeros((leaves, width), jnp.int32)
    for bit_no in range(cross_levels):
        level_no = local_levels + bit_no
        limit = jnp.where(lane // rank == bit_no, ranks[:, level_no : level_no + 1], limit)
    sums = jnp.broadcast_to(sums[:, :width], (leaves, width))
    return jnp.where(lane % rank < limit, sums, 0.0).astype(BF16)


def weights_kernel(sizes, ranks, swapped, incoming, weights):
    weights[...] = cross_weights(sizes, ranks, swapped, incoming)


def product(sizes, index_hbm, ranks, own, swap, cross, weights, blocks, right, left, near_index, extended, total, sem):
    leaves, leaf_size, cross_row = sizes["leaves"], sizes["leaf_size"], sizes["cross_row"]
    index_copy = pltpu.make_async_copy(index_hbm, near_index, sem)
    index_copy.start()
    near_part(sizes, index_copy, ranks, own, swap, cross, blocks, right, left, near_index, extended, total)
    for leaf in range(leaves):
        columns = slice(leaf * leaf_size, (leaf + 1) * leaf_size)
        far = jnp.dot(weights[...], left[cross_row:, columns], preferred_element_type=F32)
        total[leaf : leaf + 1, :] += far[leaf : leaf + 1, :]
    return total[...]


def middle_kernel(sizes, *refs):
    *inputs, slip, stress, sums, halo, near_index, extended, total, sem = refs
    right = inputs[7]
    leaf_size, cross_row = sizes["leaf_size"], sizes["cross_row"]
    first = product(sizes, *inputs, near_index, extended, total, sem)
    put_rows(stress, first)
    rows = (leaf_rows(slip) + jnp.tanh(first / 3.0)).astype(BF16)
    halo[...] = rows
    row = jnp.zeros((1, right.shape[0] - cross_row), F32)
    for leaf in range(sizes["leaves"]):
        columns = slice(leaf * leaf_size, (leaf + 1) * leaf_size)
        row += lax.dot_general(rows[leaf : leaf + 1, :], right[cross_row:, columns], NT, preferred_element_type=F32)
    sums[...] = sums_row(row)


def last_kernel(sizes, *refs):
    *inputs, first, first_stress, stress, near_index, extended, total, sem = refs
    first_stress[...] = first[...]
    put_rows(stress, product(sizes, *inputs, near_index, extended, total, sem))


def vmem(*arrays):
    return tuple(pltpu.with_memory_space_constraint(a, pltpu.VMEM) for a in arrays)


def hbm(*arrays):
    return tuple(pltpu.with_memory_space_constraint(a, pltpu.HBM) for a in arrays)


def call(kernel, out_shape, in_specs, mib, scratch=(), cost=None):
    outs = out_shape if isinstance(out_shape, tuple) else (out_shape,)
    specs = tuple(VMEM_SPEC for _ in outs)
    return pl.pallas_call(
        kernel,
        out_shape=out_shape,
        in_specs=in_specs,
        out_specs=specs if isinstance(out_shape, tuple) else specs[0],
        scratch_shapes=scratch,
        compiler_params=params(mib),
        cost_estimate=cost,
    )


def local(slip_rate, near_blocks, near_index, far_left, far_right, far_ranks):
    leaves, near, leaf_size, _ = near_blocks.shape
    levels, rank, patches = far_left.shape
    local_levels = leaves.bit_length() - 1
    devices = lax.axis_size("leaf")
    chips = devices // 2
    local_rows = local_levels * rank
    cross_rows = levels * rank - local_rows
    sizes = dict(
        leaves=leaves, near=near, leaf_size=leaf_size, rank=rank, rows=levels * rank, steps=8,
        local_levels=local_levels, cross_levels=levels - local_levels, cross_row=local_rows,
    )
    slip = slip_rate.reshape(-1, LANES)
    left = far_left.reshape(levels * rank, patches)
    right = far_right.reshape(levels * rank, patches)
    near_index = near_index.T
    sums_shape = jax.ShapeDtypeStruct((1, cross_rows + -cross_rows % LANES), F32)
    halo_shape = jax.ShapeDtypeStruct((leaves, leaf_size), BF16)
    stress_shape = jax.ShapeDtypeStruct(slip.shape, F32)
    swap = [(i, i ^ 1) for i in range(devices)]
    across = [(i, (i + 1) % devices) for i in range(1, devices, 2)]
    across += [(j, i) for i, j in across]
    groups = [[chip * 2 + core for chip in reversed(range(chips))] for core in range(2)]
    scratch = [
        pltpu.SMEM(near_index.shape, jnp.int32),
        pltpu.VMEM((3 * leaves, leaf_size), F32),
        pltpu.VMEM((leaves, leaf_size), F32),
        pltpu.SemaphoreType.DMA,
    ]
    kept = vmem(near_blocks, right, left)
    product_specs = [ANY_SPEC] + [VMEM_SPEC] * 8

    wait = pl.CostEstimate(flops=10**10, transcendentals=0, bytes_accessed=0)

    def exchange(sums, halo):
        halo_cross = lax.ppermute(halo, "leaf", across)
        halo_swap = lax.ppermute(halo, "leaf", swap)
        swapped = lax.ppermute(sums, "leaf", swap)
        outgoing = call(
            lambda *refs: spread_kernel(sizes, *refs),
            jax.ShapeDtypeStruct((chips, 1, LANES), F32),
            [VMEM_SPEC] * 2, 1, cost=wait,
        )(sums, swapped)
        incoming = lax.all_to_all(outgoing, "leaf", 0, 0, axis_index_groups=groups, tiled=True)
        weights = call(
            lambda *refs: weights_kernel(sizes, *refs),
            jax.ShapeDtypeStruct((leaves, cross_rows), BF16),
            [VMEM_SPEC] * 3, 1,
        )(far_ranks, swapped, incoming)
        return near_index, far_ranks, halo, halo_swap, halo_cross, weights, *kept

    sums, halo = call(
        lambda *refs: project_kernel(sizes, *refs),
        (sums_shape, halo_shape),
        [ANY_SPEC, ANY_SPEC], 4,
        [
            pltpu.VMEM(slip.shape, F32),
            pltpu.VMEM((cross_rows, patches), BF16),
            pltpu.SemaphoreType.DMA((sizes["steps"] + 1,)),
        ],
    )(*hbm(slip, right))
    inputs = exchange(sums, halo)
    first_stress, sums, halo = call(
        lambda *refs: middle_kernel(sizes, *refs),
        (pltpu.VMEM(slip.shape, F32), sums_shape, halo_shape),
        product_specs + [VMEM_SPEC], 4, scratch,
    )(*inputs, *vmem(slip))
    inputs = exchange(sums, halo)
    first_stress, second_stress = call(
        lambda *refs: last_kernel(sizes, *refs), (stress_shape, stress_shape), product_specs + [VMEM_SPEC], 4,
        scratch,
    )(*inputs, *vmem(first_stress))
    return (first_stress.reshape(-1), second_stress.reshape(-1))


def solution(mesh):
    in_specs = (
        P(("models", "leaf")),
        P(("models", "leaf"), None, None, None),
        P(("models", "leaf"), None),
        P(None, None, ("models", "leaf")),
        P(None, None, ("models", "leaf")),
        P(("models", "leaf"), None),
    )
    out_specs = (P(("models", "leaf")), P(("models", "leaf")))
    return jax.shard_map(local, mesh=mesh, in_specs=in_specs, out_specs=out_specs, check_vma=False)
```

time: 127 us -> 84.9 us (0.67)
  starting transfers between devices: 67 us -> 43.9 us
  waiting for transfers between devices: 37.7 us -> 19.6 us
  matrix products: 17.9 us -> 0 us
  Pallas kernels: 0 us -> 11 us
  local copies, waits for them, and re-layouts: 1.47 us -> 9.21 us
  other arithmetic: 1.49 us -> 0 us
    ppermute x18 -> x6, starting transfers between devices: 67 us -> 1.63 us  [the longest x2 1.06 us: exchange(): halo_cross = lax.ppermute(halo, 'leaf', across)]
    all_to_all x0 -> x2, starting transfers between devices: none -> 42.3 us  [exchange(): lax.all_to_all(outgoing, 'leaf', 0, 0, axis_index_groups=groups, tiled=True)]
    ppermute x18 -> x6, waiting for transfers between devices: 37.7 us -> 2.28 us  [the longest x2 2.27 us: exchange(): swapped = lax.ppermute(sums, 'leaf', swap)]
    dot_general x8 -> x0, matrix products: 17.9 us -> none  [the longest x2 9.15 us: matvec(): jnp.einsum('ikpq,ikq->ip', near_blocks, picked, preferred_element_type=jn...]
    all_to_all x0 -> x2, waiting for transfers between devices: none -> 17.3 us  [exchange(): lax.all_to_all(outgoing, 'leaf', 0, 0, axis_index_groups=groups, tiled=True)]
    pallas_call x0 -> x7, Pallas kernels: none -> 11 us  [the longest x1 3.99 us: local(): call(lambda *refs: middle_kernel(sizes, *refs), (pltpu.VMEM(slip.shape, F...]
    unnamed x36 -> x16, local copies, waits for them, and re-layouts: 0.95 us -> 9.21 us
  transfers between devices with their start and end apart: 18 -> 8, of which waited for: 14 -> 4; matrix products, arithmetic and copies ran while one was open for 8% -> 0% of each run, Pallas kernels for 0% -> 0%
where the time goes in v2:
time: 84.9 us; the launch traced here: 84.5 us
  starting transfers between devices  43.9 us (52%)
  waiting for transfers between devices  19.6 us (23%)
  Pallas kernels  11 us (13%)
  local copies, waits for them, and re-layouts  9.21 us (11%)
    all_to_all x2, starting transfers between devices, exchange(): lax.all_to_all(outgoing, 'leaf', 0, 0, axis_index_groups=groups, tiled=True)  42.3 us
    all_to_all x2, waiting for transfers between devices, exchange(): lax.all_to_all(outgoing, 'leaf', 0, 0, axis_index_groups=groups, tiled=True)  17.3 us
    unnamed x16, local copies, waits for them, and re-layouts  9.21 us
    pallas_call x1, Pallas kernels, local(): call(lambda *refs: middle_kernel(sizes, *refs), (pltpu.VMEM(slip.shape, F...  3.99 us
    pallas_call x1, Pallas kernels, local(): call(lambda *refs: last_kernel(sizes, *refs), (stress_shape, stress_shape...  3.35 us
    ppermute x2, waiting for transfers between devices, exchange(): swapped = lax.ppermute(sums, 'leaf', swap)  2.27 us
    pallas_call x1, Pallas kernels, local(): call(lambda *refs: project_kernel(sizes, *refs), (sums_shape, halo_shape)...  2.24 us
  transfers between devices with their start and end apart: 8, of which 4 were waited for; matrix products, arithmetic and copies ran while one was open for 0% of the time, Pallas kernels for 0%

profile of v2, /device:TPU:40, one launch (start us, length us, event | category | flops | bytes accessed | tf_op | source)
XLA Modules:
  0.0 84.5 jit_solution(17739962933876406753)
XLA Ops:
  0.6 2.2 %shard_map.77 = (f32[1,256]{1,0:T(1,128)S(1)}, bf16[16,256]{1,0:T(8,128)(2,1)S(1)}) custom-call(f32[32,128]{1,0:T(8,128)} %bitcast.11, bf16[352,4096]{1,0:T(8,128)(2,1)} %bitcast.6), custom_call_target="tpu_custom_call" | custom-call | tf_op jit(solution)/shard_map/pallas_call | solution.py:266
  2.9 0.0 copy-start.5
  2.9 0.1 collective-permute-start.2
  3.1 1.1 %collective-permute-done.2.refs_1_ = f32[1,256]{1,0:T(1,128)S(1)} collective-permute-done((f32[1,256]{1,0:T(1,128)S(1)}, f32[1,256]{1,0:T(1,128)S(1)}, u32[]{:S(2)}, u32[]{:S(2)}) %collective-permute-start.2) | collective-permute-done | bytes 1056 | tf_op jit(solution)/shard_map/ppermute | solution.py:252
  4.2 0.6 shard_map.78
  4.9 30.9 %all-to-all-start = ((f32[64,1,128]{2,1,0:T(1,128)}), f32[64,1,128]{2,1,0:T(1,128)S(1)}, u32[]{:S(2)}, u32[]{:S(2)}) async-start(f32[64,1,128]{2,1,0:T(1,128)} %shard_map.78), calls=%async_computation | async-start | bytes 65536 | tf_op jit(solution)/shard_map/all_to_all | solution.py:258
  35.8 0.1 collective-permute-start
  36.0 0.5 collective-permute-start.1
  36.5 8.6 %all-to-all-done.refs_2_ = f32[64,1,128]{2,1,0:T(1,128)S(1)} async-done(((f32[64,1,128]{2,1,0:T(1,128)}), f32[64,1,128]{2,1,0:T(1,128)S(1)}, u32[]{:S(2)}, u32[]{:S(2)}) %all-to-all-start) | async-done | bytes 32800 | tf_op jit(solution)/shard_map/all_to_all | solution.py:258
  45.1 0.1 shard_map.79.refs_5_
  45.3 2.8 %copy-done.1 = bf16[16,3,256,256]{3,2,1,0:T(8,128)(2,1)S(1)} copy-done((bf16[16,3,256,256]{3,2,1,0:T(8,128)(2,1)S(1)}, bf16[16,3,256,256]{3,2,1,0:T(8,128)(2,1)}, u32[]{:S(2)}) %copy-start.1) | copy-done | bytes 6291480
  48.0 1.8 %copy-done.3 = bf16[11,32,4096]{2,1,0:T(8,128)(2,1)S(1)} copy-done((bf16[11,32,4096]{2,1,0:T(8,128)(2,1)S(1)}, bf16[11,32,4096]{2,1,0:T(8,128)(2,1)}, u32[]{:S(2)}) %copy-start.3) | copy-done | bytes 2883608
  49.9 4.0 %shard_map.80 = (f32[32,128]{1,0:T(8,128)S(1)}, f32[1,256]{1,0:T(1,128)S(1)}, bf16[16,256]{1,0:T(8,128)(2,1)S(1)}) custom-call(s32[3,16]{1,0:T(4,128)S(1)} %bitcast.13, s32[16,11]{1,0:T(8,128)S(1)} %copy-done.5, bf16[16,256]{1,0:T(8,128)(2,1)S(1)} %get-tuple-element.9.refs_2_, bf16[16,256]{1,0:T(8,128)(2,1)S(1)} %collective-permute-done.refs_3_, ...), custom_call_target="tpu_custom_call" | custom-call | tf_op jit(solution)/shard_map/pallas_call | solution.py:277
  53.9 0.1 collective-permute-start.5
  54.0 1.1 %collective-permute-done.5.refs_1_ = f32[1,256]{1,0:T(1,128)S(1)} collective-permute-done((f32[1,256]{1,0:T(1,128)S(1)}, f32[1,256]{1,0:T(1,128)S(1)}, u32[]{:S(2)}, u32[]{:S(2)}) %collective-permute-start.5) | collective-permute-done | bytes 1056 | tf_op jit(solution)/shard_map/ppermute | solution.py:252
  55.1 0.6 shard_map.81
  55.8 11.3 %all-to-all-start.1 = ((f32[64,1,128]{2,1,0:T(1,128)}), f32[64,1,128]{2,1,0:T(1,128)S(1)}, u32[]{:S(2)}, u32[]{:S(2)}) async-start(f32[64,1,128]{2,1,0:T(1,128)} %shard_map.81), calls=%async_computation.1 | async-start | bytes 65536 | tf_op jit(solution)/shard_map/all_to_all | solution.py:258
  67.1 0.1 collective-permute-start.3
  67.3 0.5 collective-permute-start.4
  67.8 8.6 %all-to-all-done.1.refs_2_ = f32[64,1,128]{2,1,0:T(1,128)S(1)} async-done(((f32[64,1,128]{2,1,0:T(1,128)}), f32[64,1,128]{2,1,0:T(1,128)S(1)}, u32[]{:S(2)}, u32[]{:S(2)}) %all-to-all-start.1) | async-done | bytes 32800 | tf_op jit(solution)/shard_map/all_to_all | solution.py:258
  76.4 0.1 shard_map.82.refs_5_
  76.6 2.8 %copy-done.2 = bf16[16,3,256,256]{3,2,1,0:T(8,128)(2,1)S(1)} copy-done((bf16[16,3,256,256]{3,2,1,0:T(8,128)(2,1)S(1)}, bf16[16,3,256,256]{3,2,1,0:T(8,128)(2,1)}, u32[]{:S(2)}) %copy-start.2) | copy-done | bytes 6291480
  79.3 1.8 %copy-done.4 = bf16[11,32,4096]{2,1,0:T(8,128)(2,1)S(1)} copy-done((bf16[11,32,4096]{2,1,0:T(8,128)(2,1)S(1)}, bf16[11,32,4096]{2,1,0:T(8,128)(2,1)}, u32[]{:S(2)}) %copy-start.4) | copy-done | bytes 2883608
  81.1 3.3 %shard_map.83 = (f32[32,128]{1,0:T(8,128)}, f32[32,128]{1,0:T(8,128)}) custom-call(s32[3,16]{1,0:T(4,128)S(1)} %bitcast.14, s32[16,11]{1,0:T(8,128)S(1)} %copy-done.5, bf16[16,256]{1,0:T(8,128)(2,1)S(1)} %get-tuple-element.11.refs_2_, bf16[16,256]{1,0:T(8,128)(2,1)S(1)} %collective-permute-done.3.refs_3_, ...), custom_call_target="tpu_custom_call" | custom-call | tf_op jit(solution)/shard_map/pallas_call | solution.py:283
  (15 shorter events, 0.0 us)
Async XLA Ops:
  2.9 42.2 %copy-start.5 = (s32[16,11]{1,0:T(8,128)S(1)}, s32[16,11]{1,0:T(8,128)}, u32[]{:S(2)}) copy-start(s32[16,11]{1,0:T(8,128)} %refs_1_.3) | copy-start | bytes 2116
  2.9 42.3 %copy-start = (bf16[11,32,4096]{2,1,0:T(8,128)(2,1)S(1)}, bf16[11,32,4096]{2,1,0:T(8,128)(2,1)}, u32[]{:S(2)}) copy-start(bf16[11,32,4096]{2,1,0:T(8,128)(2,1)} %param.10) | copy-start | bytes 8650756
  2.9 42.3 %copy-start.6 = (f32[4096]{0:T(1024)S(1)}, f32[4096]{0:T(1024)}, u32[]{:S(2)}) copy-start(f32[4096]{0:T(1024)} %param.6) | copy-start | bytes 49156
  2.9 42.3 %copy-start.7 = (s32[16,3]{0,1:T(4,128)S(1)}, s32[16,3]{0,1:T(4,128)}, u32[]{:S(2)}) copy-start(s32[16,3]{0,1:T(4,128)} %param.8) | copy-start | bytes 580
  2.9 1.3 %collective-permute-start.2 = (f32[1,256]{1,0:T(1,128)S(1)}, f32[1,256]{1,0:T(1,128)S(1)}, u32[]{:S(2)}, u32[]{:S(2)}) collective-permute-start(f32[1,256]{1,0:T(1,128)S(1)} %get-tuple-element.10.refs_0_), channel_id=1, source_target_pairs={{0,1},{1,0},{2,3},{3,2},{4,5},{5,4},{6,7},{7,6},{8,9},{9,8},{10,11... | collective-permute-start | bytes 3080 | tf_op jit(solution)/shard_map/ppermute | solution.py:252
  4.9 40.3 %all-to-all-start = ((f32[64,1,128]{2,1,0:T(1,128)}), f32[64,1,128]{2,1,0:T(1,128)S(1)}, u32[]{:S(2)}, u32[]{:S(2)}) async-start(f32[64,1,128]{2,1,0:T(1,128)} %shard_map.78), calls=%async_computation | async-start | bytes 65536 | tf_op jit(solution)/shard_map/all_to_all | solution.py:258
  35.8 9.4 %collective-permute-start = (bf16[16,256]{1,0:T(8,128)(2,1)S(1)}, bf16[16,256]{1,0:T(8,128)(2,1)S(1)}, u32[]{:S(2)}, u32[]{:S(2)}) collective-permute-start(bf16[16,256]{1,0:T(8,128)(2,1)S(1)} %get-tuple-element.9.refs_2_), channel_id=1, source_target_pairs={{0,1},{1,0},{2,3},{3,2},{4,5},{5,4},{6,7},{7,6},{8,9},{9,8},{10,11... | collective-permute-start | bytes 24584 | tf_op jit(solution)/shard_map/ppermute | solution.py:251
  36.0 9.3 %collective-permute-start.1 = (bf16[16,256]{1,0:T(8,128)(2,1)S(1)}, bf16[16,256]{1,0:T(8,128)(2,1)S(1)}, u32[]{:S(2)}, u32[]{:S(2)}) collective-permute-start(bf16[16,256]{1,0:T(8,128)(2,1)S(1)} %get-tuple-element.9.refs_2_), channel_id=1, source_target_pairs={{1,2},{3,4},{5,6},{7,8},{9,10},{11,12},{13,14},{15,16},{17,18},{19... | collective-permute-start | bytes 24584 | tf_op jit(solution)/shard_map/ppermute | solution.py:250
  45.3 2.8 %copy-start.1 = (bf16[16,3,256,256]{3,2,1,0:T(8,128)(2,1)S(1)}, bf16[16,3,256,256]{3,2,1,0:T(8,128)(2,1)}, u32[]{:S(2)}) copy-start(bf16[16,3,256,256]{3,2,1,0:T(8,128)(2,1)} %refs_6_.3) | copy-start | bytes 18874372
  48.0 1.8 %copy-start.3 = (bf16[11,32,4096]{2,1,0:T(8,128)(2,1)S(1)}, bf16[11,32,4096]{2,1,0:T(8,128)(2,1)}, u32[]{:S(2)}) copy-start(bf16[11,32,4096]{2,1,0:T(8,128)(2,1)} %param.9) | copy-start | bytes 8650756
  53.9 1.3 %collective-permute-start.5 = (f32[1,256]{1,0:T(1,128)S(1)}, f32[1,256]{1,0:T(1,128)S(1)}, u32[]{:S(2)}, u32[]{:S(2)}) collective-permute-start(f32[1,256]{1,0:T(1,128)S(1)} %get-tuple-element.12.refs_0_), channel_id=1, source_target_pairs={{0,1},{1,0},{2,3},{3,2},{4,5},{5,4},{6,7},{7,6},{8,9},{9,8},{10,11... | collective-permute-start | bytes 3080 | tf_op jit(solution)/shard_map/ppermute | solution.py:252
  55.8 20.7 %all-to-all-start.1 = ((f32[64,1,128]{2,1,0:T(1,128)}), f32[64,1,128]{2,1,0:T(1,128)S(1)}, u32[]{:S(2)}, u32[]{:S(2)}) async-start(f32[64,1,128]{2,1,0:T(1,128)} %shard_map.81), calls=%async_computation.1 | async-start | bytes 65536 | tf_op jit(solution)/shard_map/all_to_all | solution.py:258
  67.1 9.4 %collective-permute-start.3 = (bf16[16,256]{1,0:T(8,128)(2,1)S(1)}, bf16[16,256]{1,0:T(8,128)(2,1)S(1)}, u32[]{:S(2)}, u32[]{:S(2)}) collective-permute-start(bf16[16,256]{1,0:T(8,128)(2,1)S(1)} %get-tuple-element.11.refs_2_), channel_id=1, source_target_pairs={{0,1},{1,0},{2,3},{3,2},{4,5},{5,4},{6,7},{7,6},{8,9},{9,8},{10,11... | collective-permute-start | bytes 24584 | tf_op jit(solution)/shard_map/ppermute | solution.py:251
  67.3 9.3 %collective-permute-start.4 = (bf16[16,256]{1,0:T(8,128)(2,1)S(1)}, bf16[16,256]{1,0:T(8,128)(2,1)S(1)}, u32[]{:S(2)}, u32[]{:S(2)}) collective-permute-start(bf16[16,256]{1,0:T(8,128)(2,1)S(1)} %get-tuple-element.11.refs_2_), channel_id=1, source_target_pairs={{1,2},{3,4},{5,6},{7,8},{9,10},{11,12},{13,14},{15,16},{17,18},{19... | collective-permute-start | bytes 24584 | tf_op jit(solution)/shard_map/ppermute | solution.py:250
  76.5 2.8 %copy-start.2 = (bf16[16,3,256,256]{3,2,1,0:T(8,128)(2,1)S(1)}, bf16[16,3,256,256]{3,2,1,0:T(8,128)(2,1)}, u32[]{:S(2)}) copy-start(bf16[16,3,256,256]{3,2,1,0:T(8,128)(2,1)} %refs_6_.3) | copy-start | bytes 18874372
  79.3 1.8 %copy-start.4 = (bf16[11,32,4096]{2,1,0:T(8,128)(2,1)S(1)}, bf16[11,32,4096]{2,1,0:T(8,128)(2,1)}, u32[]{:S(2)}) copy-start(bf16[11,32,4096]{2,1,0:T(8,128)(2,1)} %param.9) | copy-start | bytes 8650756

commit v3 on v0

v3 whole, which is shorter than its diff:
```python
import math

import jax
import jax.numpy as jnp
from jax import lax
from jax.experimental import pallas as pl
from jax.experimental.pallas import tpu as pltpu
from jax.sharding import PartitionSpec as P


F32 = jnp.float32
BF16 = jnp.bfloat16
LANES = 128
SUBLANES = 8
RING = 32
NT = (((1,), (1,)), ((), ()))
TN = (((0,), (0,)), ((), ()))
VMEM_SPEC = pl.BlockSpec(memory_space=pltpu.VMEM)
ANY_SPEC = pl.BlockSpec(memory_space=pl.ANY)


def early(devices):
    return lax.axis_index("leaf") % RING < devices


def ahead(sizes):
    return jnp.logical_and(early(sizes["ahead"]), lax.axis_index("models") + lax.axis_index("leaf") > 0)


def sums_row(total):
    total = jnp.sum(total, axis=0, keepdims=True)
    pad = -total.shape[1] % LANES
    return jnp.concatenate([total, jnp.zeros((1, pad), F32)], axis=1) if pad else total


def rows_of(ref, leaves):
    if ref.shape[1] != LANES:
        return ref[:leaves, :]
    return jnp.concatenate([ref[pl.ds(0, leaves, stride=2), :], ref[pl.ds(1, leaves, stride=2), :]], axis=1)


def put_rows(flat, rows):
    leaves = rows.shape[0]
    flat[pl.ds(0, leaves, stride=2), :] = rows[:, :LANES]
    flat[pl.ds(1, leaves, stride=2), :] = rows[:, LANES:]


def columns_of(sizes, leaf):
    return slice(leaf * sizes["leaf_size"], (leaf + 1) * sizes["leaf_size"])


def pick_row(leaf, array):
    row = lax.broadcasted_iota(jnp.int32, array.shape, 0)
    return jnp.where(row == leaf, array, 0.0)


def project_leaf(rows, factor, leaf):
    return pick_row(leaf, lax.dot_general(rows, factor, NT, preferred_element_type=F32))


def project(sizes, slip_hbm, far_right, sums, own, slip, right_cross, sems):
    leaves, steps = sizes["leaves"], sizes["steps"]
    step = leaves // steps
    cross = pl.ds(sizes["cross_row"], sizes["cross_rows"])
    copies = [pltpu.make_async_copy(slip_hbm, slip, sems.at[steps])]
    for c in range(steps):
        columns = pl.ds(c * step * sizes["leaf_size"], step * sizes["leaf_size"])
        copies.append(pltpu.make_async_copy(far_right.at[cross, columns], right_cross.at[:, columns], sems.at[c]))
    for copy in copies:
        copy.start()
    copies[0].wait()
    own[...] = rows_of(slip, leaves)
    rows = own[...].astype(BF16)
    total = jnp.zeros((leaves, right_cross.shape[0]), F32)
    for leaf in range(leaves):
        if leaf % step == 0:
            copies[1 + leaf // step].wait()
        total += project_leaf(rows, right_cross[:, columns_of(sizes, leaf)], leaf)
    sums[...] = sums_row(total)


def project_early_kernel(sizes, *refs):
    @pl.when(early(RING // 2))
    def _():
        project(sizes, *refs)


def project_late_kernel(sizes, slip_hbm, far_right, early_sums, early_own, sums, own, *scratch):
    done = early(RING // 2)

    @pl.when(done)
    def _():
        sums[...] = early_sums[...]
        own[...] = early_own[...]

    @pl.when(jnp.logical_not(done))
    def _():
        project(sizes, slip_hbm, far_right, sums, own, *scratch)


def place_of(chip, chips):
    return (chips - 1 - chips // 4 - chip) & (chips - 1)


def siblings(chip, chips, bit_no):
    start = (chip >> bit_no ^ 1) << bit_no
    return [place_of(start + step, chips) for step in range(2**bit_no)]


def lane_of(sizes, bit_no):
    return sizes["rank"] * (bit_no + 1)


def spread_kernel(sizes, own, _, outgoing):
    chip = lax.axis_index("leaf") // 2
    chips = outgoing.shape[0]
    total = own[...]
    outgoing[place_of(chip, chips)] = total[:, :LANES]
    for bit_no in range(sizes["cross_levels"] - 1):
        tile = lane_of(sizes, bit_no) // LANES * LANES
        for place in siblings(chip, chips, bit_no):
            outgoing[place] = total[:, tile : tile + LANES]


def gather_kernel(sizes, own, incoming, rows, packet):
    leaves = sizes["leaves"]
    chip = lax.axis_index("leaf") // 2
    total = own[...]
    bit_of = lax.broadcasted_iota(jnp.int32, total.shape, 1) // sizes["rank"]
    for bit_no in range(sizes["cross_levels"] - 1):
        part = sum(incoming[place] for place in siblings(chip, incoming.shape[0], bit_no))
        total = jnp.where(bit_of == 1 + bit_no, jnp.concatenate([part] * (total.shape[1] // LANES), axis=1), total)
    packet[:leaves, :] = rows_of(rows, leaves).astype(F32)
    packet[leaves:, :] = jnp.broadcast_to(total, (SUBLANES, total.shape[1]))


def far_scales(sizes, ranks, first_level, levels):
    rank, leaf_size = sizes["rank"], sizes["leaf_size"]
    shape = (sizes["leaves"], levels * rank)
    lane = lax.broadcasted_iota(jnp.int32, shape, 1)
    limit, scale = jnp.zeros(shape, jnp.int32), jnp.zeros(shape, F32)
    for number in range(levels):
        level = first_level + number
        here = lane // rank == number
        limit = jnp.where(here, ranks[:, level : level + 1], limit)
        scale = jnp.where(here, 1.0 / math.sqrt(leaf_size * 2**level), scale)
    return jnp.where(lane % rank < limit, scale, 0.0)


def own_part(sizes, ranks, own, blocks, right, left):
    leaves, local_levels, rank = sizes["leaves"], sizes["local_levels"], sizes["rank"]
    local_rows = local_levels * rank
    rows = rows_of(own, leaves).astype(BF16)
    sums = jnp.zeros((leaves, local_rows), F32)
    for leaf in range(leaves):
        sums += project_leaf(rows, right[:local_rows, columns_of(sizes, leaf)], leaf)
    total = jnp.zeros((leaves, sizes["leaf_size"]), F32)
    for leaf in range(leaves):
        total += project_leaf(rows, blocks[leaf, 0], leaf)
    row = lax.broadcasted_iota(jnp.int32, sums.shape, 0)
    level_of = lax.broadcasted_iota(jnp.int32, sums.shape, 1) // rank
    stacked = sums
    for level in range(local_levels):
        span = 2**level
        low = row // span % 2 == 0
        partner = jnp.where(low, pltpu.roll(sums, leaves - span, 0), pltpu.roll(sums, span, 0))
        stacked = jnp.where(level_of == level, partner, stacked)
        sums = sums + partner
    weights = (stacked * far_scales(sizes, ranks, 0, local_levels)).astype(BF16)
    for leaf in range(leaves):
        total += pick_row(
            leaf, jnp.dot(weights, left[:local_rows, columns_of(sizes, leaf)], preferred_element_type=F32)
        )
    return total


def other_rows(sizes, near_index, own, swap, cross):
    leaves, near = sizes["leaves"], sizes["near"]
    device = lax.axis_index("leaf")
    odd = jnp.full((leaves, sizes["leaf_size"]), device % 2) == 1
    own, swap, cross = (rows_of(ref, leaves).astype(BF16).astype(F32) for ref in (own, swap, cross))
    extended = jnp.concatenate([jnp.where(odd, swap, cross), own, jnp.where(odd, cross, swap)], axis=0).astype(BF16)
    place = near_index[...] - (device - 1) * leaves
    row = lax.broadcasted_iota(jnp.int32, (3 * leaves, leaves), 0)
    picked = jnp.concatenate([jnp.where(row == place[k : k + 1, :], 1.0, 0.0) for k in range(1, near)], axis=1)
    rows = lax.dot_general(picked.astype(BF16), extended, TN, preferred_element_type=F32).astype(BF16)
    return [rows[k * leaves : (k + 1) * leaves, :] for k in range(near - 1)]


def own_ahead_kernel(
    sizes, ranks_hbm, own, blocks_hbm, right_hbm, left_hbm, partial, ranks, blocks, right, left, sems
):
    @pl.when(ahead(sizes))
    def _():
        local_rows = pl.ds(0, right.shape[0])
        copies = [
            pltpu.make_async_copy(right_hbm.at[local_rows], right, sems.at[0]),
            pltpu.make_async_copy(left_hbm.at[local_rows], left, sems.at[1]),
            pltpu.make_async_copy(blocks_hbm.at[:, pl.ds(0, 1)], blocks, sems.at[2]),
            pltpu.make_async_copy(ranks_hbm, ranks, sems.at[3]),
        ]
        for copy in copies:
            copy.start()
        for copy in copies:
            copy.wait()
        partial[...] = own_part(sizes, ranks, own, blocks, right, left)


def own_kernel(sizes, ranks, own, blocks, right, left, before, _, partial, *scales):
    done = ahead(sizes)
    if scales:
        scales[0][...] = far_scales(sizes, ranks, sizes["local_levels"], sizes["cross_levels"])

    @pl.when(done)
    def _():
        partial[...] = before[...]

    @pl.when(jnp.logical_not(done))
    def _():
        partial[...] = own_part(sizes, ranks, own, blocks, right, left)


def product(sizes, near_index, partial, scales, own, packet, swapped, cross, blocks, left):
    leaves, cross_row, width = sizes["leaves"], sizes["cross_row"], sizes["cross_rows"]
    picked = other_rows(sizes, near_index, own, swapped, cross)
    sums, others = packet[leaves : leaves + 1, :], swapped[leaves : leaves + 1, :]
    lane = lax.broadcasted_iota(jnp.int32, sums.shape, 1)
    sums = others + jnp.where(lane < sizes["rank"], 0.0, sums)
    weights = (jnp.broadcast_to(sums[:, :width], (leaves, width)) * scales[...]).astype(BF16)
    result = partial[...]
    for leaf in range(leaves):
        result += pick_row(leaf, jnp.dot(weights, left[cross_row:, columns_of(sizes, leaf)], preferred_element_type=F32))
    for k, rows in enumerate(picked):
        for leaf in range(leaves):
            result += project_leaf(rows, blocks[leaf, 1 + k], leaf)
    return result


def middle_kernel(sizes, *refs):
    *inputs, slip, stress, halo = refs
    first = product(sizes, *inputs)
    halo[...] = (rows_of(slip, sizes["leaves"]) + jnp.tanh(first / 3.0)).astype(BF16)
    put_rows(stress, first)


def project_again(sizes, own, right, sums):
    total = jnp.zeros((sizes["leaves"], sizes["cross_rows"]), F32)
    for leaf in range(sizes["leaves"]):
        total += project_leaf(own[...], right[sizes["cross_row"] :, columns_of(sizes, leaf)], leaf)
    sums[...] = sums_row(total)


def ahead_again_kernel(sizes, ranks, own, blocks, right, left, partial, sums):
    @pl.when(early(sizes["ahead"]))
    def _():
        project_again(sizes, own, right, sums)

    @pl.when(ahead(sizes))
    def _():
        partial[...] = own_part(sizes, ranks, own, blocks, right, left)


def project_again_kernel(sizes, own, right, before, sums):
    done = early(sizes["ahead"])

    @pl.when(done)
    def _():
        sums[...] = before[...]

    @pl.when(jnp.logical_not(done))
    def _():
        project_again(sizes, own, right, sums)


def last_kernel(sizes, *refs):
    *inputs, first, first_stress, stress = refs
    first_stress[...] = first[...]
    put_rows(stress, product(sizes, *inputs))


def vmem(*arrays):
    return tuple(pltpu.with_memory_space_constraint(a, pltpu.VMEM) for a in arrays)


def hbm(*arrays):
    return tuple(pltpu.with_memory_space_constraint(a, pltpu.HBM) for a in arrays)


def local(slip_rate, near_blocks, near_index, far_left, far_right, far_ranks):
    leaves, near, leaf_size, _ = near_blocks.shape
    levels, rank, patches = far_left.shape
    local_levels = leaves.bit_length() - 1
    devices = lax.axis_size("leaf")
    chips = devices // 2
    local_rows = local_levels * rank
    cross_rows = levels * rank - local_rows
    sizes = dict(
        leaves=leaves, near=near, leaf_size=leaf_size, rank=rank, local_levels=local_levels,
        cross_levels=levels - local_levels, cross_row=local_rows, cross_rows=cross_rows, steps=2, ahead=6,
    )
    slip = slip_rate.reshape(-1, LANES)
    left = far_left.reshape(levels * rank, patches)
    right = far_right.reshape(levels * rank, patches)
    near_index = near_index.T
    shape = jax.ShapeDtypeStruct
    sums_shape = shape((1, cross_rows + -cross_rows % LANES), F32)
    partial_shape = shape((leaves, leaf_size), F32)
    stress_shape = shape(slip.shape, F32)
    swap = [(i, i ^ 1) for i in range(devices)]
    across = [(i, (i + 1) % devices) for i in range(1, devices, 2)]
    across += [(j, i) for i, j in across]
    order = sorted(range(chips), key=lambda chip: place_of(chip, chips))
    groups = [[chip * 2 + core for chip in order] for core in range(2)]

    def call(kernel, out_shape, specs, operands, mib=4, scratch=(), cost=None):
        outs = out_shape if isinstance(out_shape, tuple) else (out_shape,)
        return pl.pallas_call(
            lambda *refs: kernel(sizes, *refs),
            out_shape=out_shape,
            in_specs=specs,
            out_specs=tuple(VMEM_SPEC for _ in outs) if isinstance(out_shape, tuple) else VMEM_SPEC,
            scratch_shapes=scratch,
            compiler_params=pltpu.CompilerParams(vmem_limit_bytes=mib << 20),
            cost_estimate=cost,
        )(*operands)

    def permute(array, pairs):
        return lax.ppermute(array, "leaf", pairs)

    wait = pl.CostEstimate(flops=10**10, transcendentals=0, bytes_accessed=0)

    def exchange(sums, before, rows):
        outgoing = call(
            spread_kernel, shape((chips, 1, LANES), F32), [VMEM_SPEC, ANY_SPEC], (sums, before), 1, cost=wait
        )
        incoming = lax.all_to_all(outgoing, "leaf", 0, 0, axis_index_groups=groups, tiled=True)
        packet = call(
            gather_kernel, shape((leaves + SUBLANES, leaf_size), F32), [VMEM_SPEC] * 3, (sums, incoming, rows), 1
        )
        return packet, permute(packet, swap)

    kept = vmem(near_blocks, right, left)
    own_specs = [VMEM_SPEC] * 6 + [ANY_SPEC]
    product_specs = [VMEM_SPEC] * 9

    halo_cross = permute(slip_rate, across).reshape(-1, LANES)
    project_scratch = [
        pltpu.VMEM(slip.shape, F32),
        pltpu.VMEM((cross_rows, patches), BF16),
        pltpu.SemaphoreType.DMA((sizes["steps"] + 1,)),
    ]
    sums, own = call(
        project_early_kernel, (sums_shape, partial_shape), [ANY_SPEC] * 2, hbm(slip, right),
        scratch=project_scratch,
    )
    before = call(
        own_ahead_kernel, partial_shape, [ANY_SPEC, VMEM_SPEC] + [ANY_SPEC] * 3,
        (*hbm(far_ranks), own, *hbm(near_blocks, right, left)), 8,
        [
            pltpu.VMEM(far_ranks.shape, jnp.int32),
            pltpu.VMEM((leaves, 1, leaf_size, leaf_size), BF16),
            pltpu.VMEM((local_rows, patches), BF16),
            pltpu.VMEM((local_rows, patches), BF16),
            pltpu.SemaphoreType.DMA((4,)),
        ],
    )
    sums, own = call(
        project_late_kernel, (sums_shape, partial_shape), [ANY_SPEC] * 2 + [VMEM_SPEC] * 2,
        (*hbm(slip, right), sums, own),
        scratch=project_scratch,
    )
    packet, swapped = exchange(sums, before, own)
    partial, scales = call(
        own_kernel, (partial_shape, shape((leaves, cross_rows), F32)), own_specs,
        (far_ranks, own, *kept, before, packet),
    )
    first_stress, halo = call(
        middle_kernel, (pltpu.VMEM(slip.shape, F32), shape((leaves, leaf_size), BF16)), product_specs + [VMEM_SPEC],
        (near_index, partial, scales, own, packet, swapped, halo_cross, kept[0], kept[2], own),
    )
    halo_cross = permute(halo, across)
    before, sums = call(ahead_again_kernel, (partial_shape, sums_shape), [VMEM_SPEC] * 5, (far_ranks, halo, *kept))
    sums = call(project_again_kernel, sums_shape, [VMEM_SPEC] * 3, (halo, kept[1], sums))
    packet, swapped = exchange(sums, before, halo)
    partial = call(own_kernel, partial_shape, own_specs, (far_ranks, halo, *kept, before, packet))
    first_stress, second_stress = call(
        last_kernel, (stress_shape, stress_shape), product_specs + [VMEM_SPEC],
        (near_index, partial, scales, halo, packet, swapped, halo_cross, kept[0], kept[2], *vmem(first_stress)),
    )
    return (first_stress.reshape(-1), second_stress.reshape(-1))


def solution(mesh):
    in_specs = (
        P(("models", "leaf")),
        P(("models", "leaf"), None, None, None),
        P(("models", "leaf"), None),
        P(None, None, ("models", "leaf")),
        P(None, None, ("models", "leaf")),
        P(("models", "leaf"), None),
    )
    out_specs = (P(("models", "leaf")), P(("models", "leaf")))
    return jax.shard_map(local, mesh=mesh, in_specs=in_specs, out_specs=out_specs, check_vma=False)
```

time: 127 us -> 81.1 us (0.64)
  starting transfers between devices: 67 us -> 7.56 us
  blocking collectives: 0 us -> 55.5 us
  waiting for transfers between devices: 37.7 us -> 5.72 us
  matrix products: 17.9 us -> 0 us
  Pallas kernels: 0 us -> 11.2 us
  other arithmetic: 1.49 us -> 0.01 us
  local copies, waits for them, and re-layouts: 1.47 us -> 0.04 us
    ppermute x18 -> x4, starting transfers between devices: 67 us -> 7.56 us  [permute(): return lax.ppermute(array, 'leaf', pairs)]
    all_to_all x0 -> x2, blocking collectives: none -> 55.5 us  [exchange(): lax.all_to_all(outgoing, 'leaf', 0, 0, axis_index_groups=groups, tiled=True)]
    ppermute x18 -> x4, waiting for transfers between devices: 37.7 us -> 5.72 us  [permute(): return lax.ppermute(array, 'leaf', pairs)]
    dot_general x8 -> x0, matrix products: 17.9 us -> none  [the longest x2 9.15 us: matvec(): jnp.einsum('ikpq,ikq->ip', near_blocks, picked, preferred_element_type=jn...]
    pallas_call x0 -> x13, Pallas kernels: none -> 11.2 us  [call(): pl.pallas_call(lambda *refs: kernel(sizes, *refs), out_shape=out_shape, i...]
  transfers between devices with their start and end apart: 18 -> 4, of which waited for: 14 -> 2; matrix products, arithmetic and copies ran while one was open for 8% -> 0% of each run, Pallas kernels for 0% -> 0%
where the time goes in v3:
time: 81.1 us; the launch traced here: 80.8 us
  blocking collectives  55.5 us (68%)
  Pallas kernels  11.2 us (14%)
  starting transfers between devices  7.56 us (9%)
  waiting for transfers between devices  5.72 us (7%)
    all_to_all x2, blocking collectives, exchange(): lax.all_to_all(outgoing, 'leaf', 0, 0, axis_index_groups=groups, tiled=True)  55.5 us
    pallas_call x13, Pallas kernels, call(): pl.pallas_call(lambda *refs: kernel(sizes, *refs), out_shape=out_shape, i...  11.2 us
    ppermute x4, starting transfers between devices, permute(): return lax.ppermute(array, 'leaf', pairs)  7.56 us
    ppermute x4, waiting for transfers between devices, permute(): return lax.ppermute(array, 'leaf', pairs)  5.72 us
  transfers between devices with their start and end apart: 4, of which 2 were waited for; matrix products, arithmetic and copies ran while one was open for 0% of the time, Pallas kernels for 0%

profile of v3, /device:TPU:40, one launch (start us, length us, event | category | flops | bytes accessed | tf_op | source)
XLA Modules:
  0.0 80.8 jit_solution(15664597543058551554)
XLA Ops:
  0.6 2.0 %shard_map.77 = (f32[1,256]{1,0:T(1,128)S(1)}, f32[16,256]{1,0:T(8,128)S(1)}) custom-call(f32[32,128]{1,0:T(8,128)} %bitcast.25, bf16[352,4096]{1,0:T(8,128)(2,1)} %bitcast.9), custom_call_target="tpu_custom_call" | custom-call | tf_op jit(solution)/shard_map/pallas_call | solution.py:317
  2.7 3.4 %shard_map.79.refs_1_.refs_5_ = f32[16,256]{1,0:T(8,128)S(1)} custom-call(s32[16,11]{1,0:T(8,128)} %refs_0_.7, f32[16,256]{1,0:T(8,128)S(1)} %get-tuple-element.15.refs_3_.refs_1_, bf16[16,3,256,256]{3,2,1,0:T(8,128)(2,1)} %refs_7_.3, bf16[352,4096]{1,0:T(8,128)(2,1)} %bitcast.11, bf16[352,4096]{1,0:T(8,128)(2,1)} %bitcast.16), custom_call_target="tpu_custom_call" | custom-call | tf_op jit(solution)/shard_map/pallas_call | solution.py:317
  6.0 0.0 slice-start
  6.0 0.0 copy-start.4
  6.0 0.0 slice-start.1
  6.1 0.0 copy-start
  6.1 0.0 copy-start.1
  6.1 0.0 copy-start.2
  6.1 0.1 shard_map.80
  6.2 37.1 %all_to_all.10.refs_1_ = f32[64,1,128]{2,1,0:T(1,128)S(1)} all-to-all(f32[64,1,128]{2,1,0:T(1,128)S(1)} %shard_map.80), channel_id=1, replica_groups={{94,92,90,88,86,84,82,80,78,76,74,72,70,68,66,64,62,60,58,56,54,52,50,4..., dimensions={0} | all-to-all | bytes 65536 | tf_op jit(solution)/shard_map/all_to_all | solution.py:336
  43.3 0.0 copy-start.3
  43.3 0.1 collective-permute-start
  43.5 3.7 %collective-permute-start.1 = (f32[4096]{0:T(1024)S(1)}, f32[4096]{0:T(1024)S(1)}, u32[]{:S(2)}, u32[]{:S(2)}) collective-permute-start(f32[4096]{0:T(1024)S(1)} %copy-done.4), channel_id=1, source_target_pairs={{1,2},{3,4},{5,6},{7,8},{9,10},{11,12},{13,14},{15,16},{17,18},{19... | collective-permute-start | bytes 49160 | tf_op jit(solution)/shard_map/ppermute | solution.py:328
  47.2 0.1 shard_map.82
  47.3 2.8 %collective-permute-done.1 = f32[4096]{0:T(1024)S(1)} collective-permute-done((f32[4096]{0:T(1024)S(1)}, f32[4096]{0:T(1024)S(1)}, u32[]{:S(2)}, u32[]{:S(2)}) %collective-permute-start.1) | collective-permute-done | bytes 16416 | tf_op jit(solution)/shard_map/ppermute | solution.py:328
  50.1 0.0 collective-permute-done.refs_5_
  50.1 1.5 %shard_map.83 = (f32[32,128]{1,0:T(8,128)S(1)}, bf16[16,256]{1,0:T(8,128)(2,1)S(1)}) custom-call(s32[3,16]{1,0:T(4,128)S(1)} %bitcast.23, f32[16,256]{1,0:T(8,128)S(1)} %get-tuple-element.18.refs_1_, f32[16,224]{1,0:T(8,128)S(1)} %get-tuple-element.19.refs_2_, f32[16,256]{1,0:T(8,128)S(1)} %get-tuple-element.16.refs_2_.refs_1_.refs_3_.refs_9_, ...), custom_call_target="tpu_custom_call" | custom-call | tf_op jit(solution)/shard_map/pallas_call | solution.py:317
  51.6 1.7 %shard_map.84 = (f32[16,256]{1,0:T(8,128)S(1)}, f32[1,256]{1,0:T(1,128)S(1)}) custom-call(s32[16,11]{1,0:T(8,128)S(1)} %copy-done.2, bf16[16,256]{1,0:T(8,128)(2,1)S(1)} %get-tuple-element.20.refs_1_.refs_0_.refs_2_.refs_3_, bf16[16,3,256,256]{3,2,1,0:T(8,128)(2,1)S(1)} %bitcast.8, bf16[352,4096]{1,0:T(8,128)(2,1)S(1)} %bitcast.13, ...), custom_call_target="tpu_custom_call" | custom-call | tf_op jit(solution)/shard_map/pallas_call | solution.py:317
  53.4 0.1 shard_map.86
  53.5 18.5 %all_to_all.11.refs_1_ = f32[64,1,128]{2,1,0:T(1,128)S(1)} all-to-all(f32[64,1,128]{2,1,0:T(1,128)S(1)} %shard_map.86), channel_id=1, replica_groups={{94,92,90,88,86,84,82,80,78,76,74,72,70,68,66,64,62,60,58,56,54,52,50,4..., dimensions={0} | all-to-all | bytes 65536 | tf_op jit(solution)/shard_map/all_to_all | solution.py:336
  72.0 0.1 collective-permute-start.2
  72.1 3.6 %collective-permute-start.3 = (bf16[16,256]{1,0:T(8,128)(2,1)S(1)}, bf16[16,256]{1,0:T(8,128)(2,1)S(1)}, u32[]{:S(2)}, u32[]{:S(2)}) collective-permute-start(bf16[16,256]{1,0:T(8,128)(2,1)S(1)} %get-tuple-element.20.refs_1_.refs_0_.refs_2_.refs_3_), channel_id=1, source_target_pairs={{1,2},{3,4},{5,6},{7,8},{9,10},{11,12},{13,14},{15,16},{17,18},{19... | collective-permute-start | bytes 24584 | tf_op jit(solution)/shard_map/ppermute | solution.py:328
  75.8 2.9 %collective-permute-done.3.refs_6_ = bf16[16,256]{1,0:T(8,128)(2,1)S(1)} collective-permute-done((bf16[16,256]{1,0:T(8,128)(2,1)S(1)}, bf16[16,256]{1,0:T(8,128)(2,1)S(1)}, u32[]{:S(2)}, u32[]{:S(2)}) %collective-permute-start.3) | collective-permute-done | bytes 8224 | tf_op jit(solution)/shard_map/ppermute | solution.py:328
  78.6 2.2 %shard_map.89 = (f32[32,128]{1,0:T(8,128)}, f32[32,128]{1,0:T(8,128)}) custom-call(s32[3,16]{1,0:T(4,128)S(1)} %bitcast.24, f32[16,256]{1,0:T(8,128)S(1)} %shard_map.88.refs_1_, f32[16,224]{1,0:T(8,128)S(1)} %get-tuple-element.19.refs_2_, bf16[16,256]{1,0:T(8,128)(2,1)S(1)} %get-tuple-element.20.refs_1_.refs_0_.refs_2_.refs_3_, ...), custom_call_target="tpu_custom_call" | custom-call | tf_op jit(solution)/shard_map/pallas_call | solution.py:317
  (14 shorter events, 0.2 us)
Async XLA Ops:
  6.0 41.1 %slice-start = ((s8[6291456]{0:T(1024)(128)(4,1)}), s8[4194304]{0:T(1024)(128)(4,1)S(1)}, s32[]{:S(2)}) async-start(s8[6291456]{0:T(1024)(128)(4,1)} %bitcast.7), calls=%async_computation.2 | async-start | bytes 8388608
  6.0 37.4 %copy-start.4 = (f32[4096]{0:T(1024)S(1)}, f32[4096]{0:T(1024)}, u32[]{:S(2)}) copy-start(f32[4096]{0:T(1024)} %param.6) | copy-start | bytes 49156
  6.0 41.1 %slice-start.1 = ((s8[6291456]{0:T(1024)(128)(4,1)}), s8[2097152]{0:T(1024)(128)(4,1)S(1)}, s32[]{:S(2)}) async-start(s8[6291456]{0:T(1024)(128)(4,1)} %bitcast.7), calls=%async_computation.3 | async-start | bytes 4194304
  6.1 41.1 %copy-start = (bf16[11,32,4096]{2,1,0:T(8,128)(2,1)S(1)}, bf16[11,32,4096]{2,1,0:T(8,128)(2,1)}, u32[]{:S(2)}) copy-start(bf16[11,32,4096]{2,1,0:T(8,128)(2,1)} %param.10) | copy-start | bytes 8650756
  6.1 41.1 %copy-start.1 = (bf16[11,32,4096]{2,1,0:T(8,128)(2,1)S(1)}, bf16[11,32,4096]{2,1,0:T(8,128)(2,1)}, u32[]{:S(2)}) copy-start(bf16[11,32,4096]{2,1,0:T(8,128)(2,1)} %param.9) | copy-start | bytes 8650756
  6.1 41.1 %copy-start.2 = (s32[16,11]{1,0:T(8,128)S(1)}, s32[16,11]{1,0:T(8,128)}, u32[]{:S(2)}) copy-start(s32[16,11]{1,0:T(8,128)} %refs_0_.7) | copy-start | bytes 2116
  43.3 6.8 %copy-start.3 = (s32[16,3]{0,1:T(4,128)S(1)}, s32[16,3]{0,1:T(4,128)}, u32[]{:S(2)}) copy-start(s32[16,3]{0,1:T(4,128)} %param.8) | copy-start | bytes 580
  43.3 6.8 %collective-permute-start = (f32[24,256]{1,0:T(8,128)S(1)}, f32[24,256]{1,0:T(8,128)S(1)}, u32[]{:S(2)}, u32[]{:S(2)}) collective-permute-start(f32[24,256]{1,0:T(8,128)S(1)} %shard_map.81.refs_6_.refs_4_), channel_id=1, source_target_pairs={{0,1},{1,0},{2,3},{3,2},{4,5},{5,4},{6,7},{7,6},{8,9},{9,8},{10,11... | collective-permute-start | bytes 73736 | tf_op jit(solution)/shard_map/ppermute | solution.py:328
  43.5 6.6 %collective-permute-start.1 = (f32[4096]{0:T(1024)S(1)}, f32[4096]{0:T(1024)S(1)}, u32[]{:S(2)}, u32[]{:S(2)}) collective-permute-start(f32[4096]{0:T(1024)S(1)} %copy-done.4), channel_id=1, source_target_pairs={{1,2},{3,4},{5,6},{7,8},{9,10},{11,12},{13,14},{15,16},{17,18},{19... | collective-permute-start | bytes 49160 | tf_op jit(solution)/shard_map/ppermute | solution.py:328
  72.0 6.7 %collective-permute-start.2 = (f32[24,256]{1,0:T(8,128)S(1)}, f32[24,256]{1,0:T(8,128)S(1)}, u32[]{:S(2)}, u32[]{:S(2)}) collective-permute-start(f32[24,256]{1,0:T(8,128)S(1)} %shard_map.87.refs_6_.refs_4_), channel_id=1, source_target_pairs={{0,1},{1,0},{2,3},{3,2},{4,5},{5,4},{6,7},{7,6},{8,9},{9,8},{10,11... | collective-permute-start | bytes 73736 | tf_op jit(solution)/shard_map/ppermute | solution.py:328
  72.1 6.5 %collective-permute-start.3 = (bf16[16,256]{1,0:T(8,128)(2,1)S(1)}, bf16[16,256]{1,0:T(8,128)(2,1)S(1)}, u32[]{:S(2)}, u32[]{:S(2)}) collective-permute-start(bf16[16,256]{1,0:T(8,128)(2,1)S(1)} %get-tuple-element.20.refs_1_.refs_0_.refs_2_.refs_3_), channel_id=1, source_target_pairs={{1,2},{3,4},{5,6},{7,8},{9,10},{11,12},{13,14},{15,16},{17,18},{19... | collective-permute-start | bytes 24584 | tf_op jit(solution)/shard_map/ppermute | solution.py:328

commit v4 on v3

--- a/solution.py
+++ b/solution.py
@@ -122,7 +122,7 @@
             outgoing[place] = total[:, tile : tile + LANES]
 
 
-def gather_kernel(sizes, own, incoming, rows, packet):
+def gather_kernel(sizes, own, incoming, *refs):
     leaves = sizes["leaves"]
     chip = lax.axis_index("leaf") // 2
     total = own[...]
@@ -130,8 +130,11 @@
     for bit_no in range(sizes["cross_levels"] - 1):
         part = sum(incoming[place] for place in siblings(chip, incoming.shape[0], bit_no))
         total = jnp.where(bit_of == 1 + bit_no, jnp.concatenate([part] * (total.shape[1] // LANES), axis=1), total)
-    packet[:leaves, :] = rows_of(rows, leaves).astype(F32)
-    packet[leaves:, :] = jnp.broadcast_to(total, (SUBLANES, total.shape[1]))
+    *rows, packet = refs
+    if rows:
+        packet[:leaves, :] = rows_of(rows[0], leaves).astype(F32)
+        total = jnp.broadcast_to(total, (SUBLANES, total.shape[1]))
+    packet[packet.shape[0] - total.shape[0] :, :] = total
 
 
 def far_scales(sizes, ranks, first_level, levels):
@@ -206,10 +209,12 @@
         partial[...] = own_part(sizes, ranks, own, blocks, right, left)
 
 
-def own_kernel(sizes, ranks, own, blocks, right, left, before, _, partial, *scales):
+def second_core():
+    return lax.axis_index("leaf") % 2 == 1
+
+
+def own_or_before(sizes, ranks, own, blocks, right, left, before, partial):
     done = ahead(sizes)
-    if scales:
-        scales[0][...] = far_scales(sizes, ranks, sizes["local_levels"], sizes["cross_levels"])
 
     @pl.when(done)
     def _():
@@ -220,25 +225,57 @@
         partial[...] = own_part(sizes, ranks, own, blocks, right, left)
 
 
-def product(sizes, near_index, partial, scales, own, packet, swapped, cross, blocks, left):
+def own_second_kernel(sizes, ranks, own, blocks, right, left, before, packet, partial, packet_out):
+    packet_out[...] = packet[...]
+
+    @pl.when(second_core())
+    def _():
+        own_or_before(sizes, ranks, own, blocks, right, left, before, partial)
+
+
+def own_first_kernel(sizes, ranks, own, blocks, right, left, before, second, _, partial, scales):
+    scales[...] = far_scales(sizes, ranks, sizes["local_levels"], sizes["cross_levels"])
+
+    @pl.when(second_core())
+    def _():
+        partial[...] = second[...]
+
+    @pl.when(jnp.logical_not(second_core()))
+    def _():
+        own_or_before(sizes, ranks, own, blocks, right, left, before, partial)
+
+
+def other_part(sizes, picked, blocks):
+    total = jnp.zeros((sizes["leaves"], sizes["leaf_size"]), F32)
+    for k, rows in enumerate(picked):
+        for leaf in range(sizes["leaves"]):
+            total += project_leaf(rows, blocks[leaf, 1 + k], leaf)
+    return total
+
+
+def near_kernel(sizes, near_index, ranks, own, swap, cross, blocks, right, left, before, _, partial):
+    picked = other_rows(sizes, near_index, own, swap, cross)
+    own_or_before(sizes, ranks, own, blocks, right, left, before, partial)
+    partial[...] += other_part(sizes, picked, blocks)
+
+
+def cross_part(sizes, scales, packet, swapped, left):
     leaves, cross_row, width = sizes["leaves"], sizes["cross_row"], sizes["cross_rows"]
-    picked = other_rows(sizes, near_index, own, swapped, cross)
-    sums, others = packet[leaves : leaves + 1, :], swapped[leaves : leaves + 1, :]
+    sums, others = packet[packet.shape[0] - 1 :, :], swapped[swapped.shape[0] - 1 :, :]
     lane = lax.broadcasted_iota(jnp.int32, sums.shape, 1)
     sums = others + jnp.where(lane < sizes["rank"], 0.0, sums)
     weights = (jnp.broadcast_to(sums[:, :width], (leaves, width)) * scales[...]).astype(BF16)
-    result = partial[...]
+    total = jnp.zeros((leaves, sizes["leaf_size"]), F32)
     for leaf in range(leaves):
-        result += pick_row(leaf, jnp.dot(weights, left[cross_row:, columns_of(sizes, leaf)], preferred_element_type=F32))
-    for k, rows in enumerate(picked):
-        for leaf in range(leaves):
-            result += project_leaf(rows, blocks[leaf, 1 + k], leaf)
-    return result
-
-
-def middle_kernel(sizes, *refs):
-    *inputs, slip, stress, halo = refs
-    first = product(sizes, *inputs)
+        total += pick_row(leaf, jnp.dot(weights, left[cross_row:, columns_of(sizes, leaf)], preferred_element_type=F32))
+    return total
+
+
+def middle_kernel(
+    sizes, near_index, partial, scales, own, packet, swapped, cross, blocks, left, slip, stress, halo
+):
+    picked = other_rows(sizes, near_index, own, swapped, cross)
+    first = partial[...] + cross_part(sizes, scales, packet, swapped, left) + other_part(sizes, picked, blocks)
     halo[...] = (rows_of(slip, sizes["leaves"]) + jnp.tanh(first / 3.0)).astype(BF16)
     put_rows(stress, first)
 
@@ -272,10 +309,9 @@
         project_again(sizes, own, right, sums)
 
 
-def last_kernel(sizes, *refs):
-    *inputs, first, first_stress, stress = refs
+def last_kernel(sizes, partial, scales, packet, swapped, left, first, first_stress, stress):
     first_stress[...] = first[...]
-    put_rows(stress, product(sizes, *inputs))
+    put_rows(stress, partial[...] + cross_part(sizes, scales, packet, swapped, left))
 
 
 def vmem(*arrays):
@@ -296,7 +332,7 @@
     cross_rows = levels * rank - local_rows
     sizes = dict(
         leaves=leaves, near=near, leaf_size=leaf_size, rank=rank, local_levels=local_levels,
-        cross_levels=levels - local_levels, cross_row=local_rows, cross_rows=cross_rows, steps=2, ahead=6,
+        cross_levels=levels - local_levels, cross_row=local_rows, cross_rows=cross_rows, steps=2, ahead=2,
     )
     slip = slip_rate.reshape(-1, LANES)
     left = far_left.reshape(levels * rank, patches)
@@ -329,18 +365,18 @@
 
     wait = pl.CostEstimate(flops=10**10, transcendentals=0, bytes_accessed=0)
 
-    def exchange(sums, before, rows):
+    def exchange(sums, before, *rows):
         outgoing = call(
             spread_kernel, shape((chips, 1, LANES), F32), [VMEM_SPEC, ANY_SPEC], (sums, before), 1, cost=wait
         )
         incoming = lax.all_to_all(outgoing, "leaf", 0, 0, axis_index_groups=groups, tiled=True)
         packet = call(
-            gather_kernel, shape((leaves + SUBLANES, leaf_size), F32), [VMEM_SPEC] * 3, (sums, incoming, rows), 1
+            gather_kernel, shape((leaves + SUBLANES, leaf_size), F32) if rows else sums_shape,
+            [VMEM_SPEC] * (2 + len(rows)), (sums, incoming, *rows), 1,
         )
-        return packet, permute(packet, swap)
+        return packet
 
     kept = vmem(near_blocks, right, left)
-    own_specs = [VMEM_SPEC] * 6 + [ANY_SPEC]
     product_specs = [VMEM_SPEC] * 9
 
     halo_cross = permute(slip_rate, across).reshape(-1, LANES)
@@ -369,23 +405,33 @@
         (*hbm(slip, right), sums, own),
         scratch=project_scratch,
     )
-    packet, swapped = exchange(sums, before, own)
+    packet = exchange(sums, before, own)
+    second, packet = call(
+        own_second_kernel, (partial_shape, shape(packet.shape, F32)), [VMEM_SPEC] * 7,
+        (far_ranks, own, *kept, before, packet),
+    )
+    swapped = permute(packet, swap)
     partial, scales = call(
-        own_kernel, (partial_shape, shape((leaves, cross_rows), F32)), own_specs,
-        (far_ranks, own, *kept, before, packet),
+        own_first_kernel, (partial_shape, shape((leaves, cross_rows), F32)), [VMEM_SPEC] * 7 + [ANY_SPEC],
+        (far_ranks, own, *kept, before, second, packet),
     )
     first_stress, halo = call(
         middle_kernel, (pltpu.VMEM(slip.shape, F32), shape((leaves, leaf_size), BF16)), product_specs + [VMEM_SPEC],
         (near_index, partial, scales, own, packet, swapped, halo_cross, kept[0], kept[2], own),
     )
     halo_cross = permute(halo, across)
+    halo_swap = permute(halo, swap)
     before, sums = call(ahead_again_kernel, (partial_shape, sums_shape), [VMEM_SPEC] * 5, (far_ranks, halo, *kept))
     sums = call(project_again_kernel, sums_shape, [VMEM_SPEC] * 3, (halo, kept[1], sums))
-    packet, swapped = exchange(sums, before, halo)
-    partial = call(own_kernel, partial_shape, own_specs, (far_ranks, halo, *kept, before, packet))
+    packet = exchange(sums, before)
+    swapped = permute(packet, swap)
+    partial = call(
+        near_kernel, partial_shape, [VMEM_SPEC] * 9 + [ANY_SPEC],
+        (near_index, far_ranks, halo, halo_swap, halo_cross, *kept, before, packet),
+    )
     first_stress, second_stress = call(
-        last_kernel, (stress_shape, stress_shape), product_specs + [VMEM_SPEC],
-        (near_index, partial, scales, halo, packet, swapped, halo_cross, kept[0], kept[2], *vmem(first_stress)),
+        last_kernel, (stress_shape, stress_shape), [VMEM_SPEC] * 6,
+        (partial, scales, packet, swapped, kept[2], *vmem(first_stress)),
     )
     return (first_stress.reshape(-1), second_stress.reshape(-1))
 

time: 81.1 us -> 81.4 us (level)
  blocking collectives: 55.5 us -> 37.1 us
  waiting for transfers between devices: 5.72 us -> 12.2 us
  starting transfers between devices: 7.56 us -> 13 us
  local copies, waits for them, and re-layouts: 0.04 us -> 5.16 us
    all_to_all x2 -> x1, blocking collectives: 55.5 us -> 37.1 us  [exchange(): lax.all_to_all(outgoing, 'leaf', 0, 0, axis_index_groups=groups, tiled=True)]
    all_to_all x0 -> x1, waiting for transfers between devices: none -> 8.95 us  [exchange(): lax.all_to_all(outgoing, 'leaf', 0, 0, axis_index_groups=groups, tiled=True)]
    all_to_all x0 -> x1, starting transfers between devices: none -> 8.82 us  [exchange(): lax.all_to_all(outgoing, 'leaf', 0, 0, axis_index_groups=groups, tiled=True)]
    unnamed x14 -> x18, local copies, waits for them, and re-layouts: 0.04 us -> 5.16 us
    ppermute x4 -> x5, starting transfers between devices: 7.56 us -> 4.22 us  [permute(): return lax.ppermute(array, 'leaf', pairs)]
    ppermute x4 -> x5, waiting for transfers between devices: 5.72 us -> 3.26 us  [permute(): return lax.ppermute(array, 'leaf', pairs)]
    pallas_call x13 -> x14, Pallas kernels: 11.2 us -> 12 us  [call(): pl.pallas_call(lambda *refs: kernel(sizes, *refs), out_shape=out_shape, i...]
  transfers between devices with their start and end apart: 4 -> 6, of which waited for: 2 -> 2; matrix products, arithmetic and copies ran while one was open for 0% -> 0% of each run, Pallas kernels for 0% -> 2%
where the time goes in v4:
time: 81.4 us; the launch traced here: 80.4 us
  blocking collectives  37.1 us (46%)
  starting transfers between devices  13 us (16%)
  waiting for transfers between devices  12.2 us (15%)
  Pallas kernels  12 us (15%)
  local copies, waits for them, and re-layouts  5.16 us (6%)
  between operations  0.93 us (1%)
    all_to_all x1, blocking collectives, exchange(): lax.all_to_all(outgoing, 'leaf', 0, 0, axis_index_groups=groups, tiled=True)  37.1 us
    pallas_call x14, Pallas kernels, call(): pl.pallas_call(lambda *refs: kernel(sizes, *refs), out_shape=out_shape, i...  12 us
    all_to_all x1, waiting for transfers between devices, exchange(): lax.all_to_all(outgoing, 'leaf', 0, 0, axis_index_groups=groups, tiled=True)  8.95 us
    all_to_all x1, starting transfers between devices, exchange(): lax.all_to_all(outgoing, 'leaf', 0, 0, axis_index_groups=groups, tiled=True)  8.82 us
    unnamed x18, local copies, waits for them, and re-layouts  5.16 us
    ppermute x5, starting transfers between devices, permute(): return lax.ppermute(array, 'leaf', pairs)  4.22 us
    ppermute x5, waiting for transfers between devices, permute(): return lax.ppermute(array, 'leaf', pairs)  3.26 us
  transfers between devices with their start and end apart: 6, of which 2 were waited for; matrix products, arithmetic and copies ran while one was open for 0% of the time, Pallas kernels for 2%

profile of v4, /device:TPU:40, one launch (start us, length us, event | category | flops | bytes accessed | tf_op | source)
XLA Modules:
  0.0 80.4 jit_solution(4495692168320218936)
XLA Ops:
  0.6 2.0 %shard_map.77 = (f32[1,256]{1,0:T(1,128)S(1)}, f32[16,256]{1,0:T(8,128)S(1)}) custom-call(f32[32,128]{1,0:T(8,128)} %bitcast.27, bf16[352,4096]{1,0:T(8,128)(2,1)} %bitcast.9), custom_call_target="tpu_custom_call" | custom-call | tf_op jit(solution)/shard_map/pallas_call | solution.py:353
  2.7 3.4 %shard_map.79.refs_1_.refs_5_ = f32[16,256]{1,0:T(8,128)S(1)} custom-call(s32[16,11]{1,0:T(8,128)} %refs_1_.1, f32[16,256]{1,0:T(8,128)S(1)} %get-tuple-element.17.refs_3_.refs_1_, bf16[16,3,256,256]{3,2,1,0:T(8,128)(2,1)} %refs_5_.1, bf16[352,4096]{1,0:T(8,128)(2,1)} %bitcast.11, bf16[352,4096]{1,0:T(8,128)(2,1)} %bitcast.17), custom_call_target="tpu_custom_call" | custom-call | tf_op jit(solution)/shard_map/pallas_call | solution.py:353
  6.0 0.0 slice-start
  6.0 0.0 copy-start.1
  6.1 0.1 shard_map.80
  6.2 37.1 %all_to_all.10.refs_1_ = f32[64,1,128]{2,1,0:T(1,128)S(1)} all-to-all(f32[64,1,128]{2,1,0:T(1,128)S(1)} %shard_map.80), channel_id=1, replica_groups={{94,92,90,88,86,84,82,80,78,76,74,72,70,68,66,64,62,60,58,56,54,52,50,4..., dimensions={0} | all-to-all | bytes 65536 | tf_op jit(solution)/shard_map/all_to_all | solution.py:372
  43.4 0.1 collective-permute-start
  43.5 0.5 copy-done.6
  44.1 3.1 %collective-permute-start.1 = (f32[4096]{0:T(1024)S(1)}, f32[4096]{0:T(1024)S(1)}, u32[]{:S(2)}, u32[]{:S(2)}) collective-permute-start(f32[4096]{0:T(1024)S(1)} %copy-done.6), channel_id=1, source_target_pairs={{1,2},{3,4},{5,6},{7,8},{9,10},{11,12},{13,14},{15,16},{17,18},{19... | collective-permute-start | bytes 49160 | tf_op jit(solution)/shard_map/ppermute | solution.py:364
  47.2 0.1 shard_map.83
  47.3 3.3 %collective-permute-done.1 = f32[4096]{0:T(1024)S(1)} collective-permute-done((f32[4096]{0:T(1024)S(1)}, f32[4096]{0:T(1024)S(1)}, u32[]{:S(2)}, u32[]{:S(2)}) %collective-permute-start.1) | collective-permute-done | bytes 16416 | tf_op jit(solution)/shard_map/ppermute | solution.py:364
  50.6 1.5 %shard_map.84 = (f32[32,128]{1,0:T(8,128)S(1)}, bf16[16,256]{1,0:T(8,128)(2,1)S(1)}) custom-call(s32[3,16]{1,0:T(4,128)S(1)} %bitcast.25, f32[16,256]{1,0:T(8,128)S(1)} %get-tuple-element.22.refs_1_, f32[16,224]{1,0:T(8,128)S(1)} %get-tuple-element.23.refs_2_.refs_1_, f32[16,256]{1,0:T(8,128)S(1)} %get-tuple-element.18.refs_2_.refs_1_.refs_3_.refs_9_, ...), custom_call_target="tpu_custom_call" | custom-call | tf_op jit(solution)/shard_map/pallas_call | solution.py:353
  52.1 1.7 %shard_map.85 = (f32[16,256]{1,0:T(8,128)S(1)}, f32[1,256]{1,0:T(1,128)S(1)}) custom-call(s32[16,11]{1,0:T(8,128)S(1)} %copy-done.4, bf16[16,256]{1,0:T(8,128)(2,1)S(1)} %get-tuple-element.24.refs_1_.refs_0_.refs_2_, bf16[16,3,256,256]{3,2,1,0:T(8,128)(2,1)S(1)} %bitcast.8, bf16[352,4096]{1,0:T(8,128)(2,1)S(1)} %bitcast.14, bf16[352,4096]{1,0:T(8,128)(2,1)S(1)} %bitcast.21), custom_call_target="tpu_custom_call" | custom-call | tf_op jit(solution)/shard_map/pallas_call | solution.py:353
  53.9 0.7 shard_map.87
  54.6 8.8 %all-to-all-start.1 = ((f32[64,1,128]{2,1,0:T(1,128)}), f32[64,1,128]{2,1,0:T(1,128)S(1)}, u32[]{:S(2)}, u32[]{:S(2)}) async-start(f32[64,1,128]{2,1,0:T(1,128)} %shard_map.87), calls=%async_computation.1 | async-start | bytes 65536 | tf_op jit(solution)/shard_map/all_to_all | solution.py:372
  63.4 0.1 collective-permute-start.2
  63.5 0.7 collective-permute-start.3
  64.2 9.0 %all-to-all-done.1.refs_1_ = f32[64,1,128]{2,1,0:T(1,128)S(1)} async-done(((f32[64,1,128]{2,1,0:T(1,128)}), f32[64,1,128]{2,1,0:T(1,128)S(1)}, u32[]{:S(2)}, u32[]{:S(2)}) %all-to-all-start.1) | async-done | bytes 32800 | tf_op jit(solution)/shard_map/all_to_all | solution.py:372
  73.2 0.1 shard_map.88.refs_9_.refs_2_
  73.2 0.1 collective-permute-start.4
  73.4 2.8 %copy-done = bf16[16,3,256,256]{3,2,1,0:T(8,128)(2,1)S(1)} copy-done((bf16[16,3,256,256]{3,2,1,0:T(8,128)(2,1)S(1)}, bf16[16,3,256,256]{3,2,1,0:T(8,128)(2,1)}, u32[]{:S(2)}) %copy-start) | copy-done | bytes 6291480
  76.2 1.8 %copy-done.3 = bf16[11,32,4096]{2,1,0:T(8,128)(2,1)S(1)} copy-done((bf16[11,32,4096]{2,1,0:T(8,128)(2,1)S(1)}, bf16[11,32,4096]{2,1,0:T(8,128)(2,1)}, u32[]{:S(2)}) %copy-start.3) | copy-done | bytes 2883608
  78.0 1.4 %shard_map.89.refs_0_ = f32[16,256]{1,0:T(8,128)S(1)} custom-call(s32[3,16]{1,0:T(4,128)S(1)} %bitcast.26, s32[16,11]{1,0:T(8,128)S(1)} %copy-done.4, bf16[16,256]{1,0:T(8,128)(2,1)S(1)} %get-tuple-element.24.refs_1_.refs_0_.refs_2_, bf16[16,256]{1,0:T(8,128)(2,1)S(1)} %collective-permute-done.2.refs_3_, bf16[16,256]{1,0:T(8,128)(2,1)S(1)} %collective-permute-done.3.refs_4_, ...), custom_call_target="tpu_custom_call" | custom-call | tf_op jit(solution)/shard_map/pallas_call | solution.py:353
  79.4 1.0 %shard_map.90 = (f32[32,128]{1,0:T(8,128)}, f32[32,128]{1,0:T(8,128)}) custom-call(f32[16,256]{1,0:T(8,128)S(1)} %shard_map.89.refs_0_, f32[16,224]{1,0:T(8,128)S(1)} %get-tuple-element.23.refs_2_.refs_1_, f32[1,256]{1,0:T(1,128)S(1)} %shard_map.88.refs_9_.refs_2_, f32[1,256]{1,0:T(1,128)S(1)} %collective-permute-done.4.refs_3_, ...), custom_call_target="tpu_custom_call" | custom-call | tf_op jit(solution)/shard_map/pallas_call | solution.py:353
  (22 shorter events, 0.2 us)
Async XLA Ops:
  6.0 37.3 %slice-start = ((s8[6291456]{0:T(1024)(128)(4,1)}), s8[4194304]{0:T(1024)(128)(4,1)S(1)}, s32[]{:S(2)}) async-start(s8[6291456]{0:T(1024)(128)(4,1)} %bitcast.7), calls=%async_computation.2 | async-start | bytes 8388608
  6.0 37.3 %slice-start.1 = ((s8[6291456]{0:T(1024)(128)(4,1)}), s8[2097152]{0:T(1024)(128)(4,1)S(1)}, s32[]{:S(2)}) async-start(s8[6291456]{0:T(1024)(128)(4,1)} %bitcast.7), calls=%async_computation.3 | async-start | bytes 4194304
  6.0 37.3 %copy-start.1 = (bf16[11,32,4096]{2,1,0:T(8,128)(2,1)S(1)}, bf16[11,32,4096]{2,1,0:T(8,128)(2,1)}, u32[]{:S(2)}) copy-start(bf16[11,32,4096]{2,1,0:T(8,128)(2,1)} %param.10) | copy-start | bytes 8650756
  6.1 37.3 %copy-start.2 = (bf16[11,32,4096]{2,1,0:T(8,128)(2,1)S(1)}, bf16[11,32,4096]{2,1,0:T(8,128)(2,1)}, u32[]{:S(2)}) copy-start(bf16[11,32,4096]{2,1,0:T(8,128)(2,1)} %param.9) | copy-start | bytes 8650756
  6.1 37.3 %copy-start.4 = (s32[16,11]{1,0:T(8,128)S(1)}, s32[16,11]{1,0:T(8,128)}, u32[]{:S(2)}) copy-start(s32[16,11]{1,0:T(8,128)} %refs_1_.1) | copy-start | bytes 2116
  43.3 0.7 copy-start.6
  43.4 7.2 %collective-permute-start = (f32[24,256]{1,0:T(8,128)S(1)}, f32[24,256]{1,0:T(8,128)S(1)}, u32[]{:S(2)}, u32[]{:S(2)}) collective-permute-start(f32[24,256]{1,0:T(8,128)S(1)} %get-tuple-element.21.refs_7_.refs_4_), channel_id=1, source_target_pairs={{0,1},{1,0},{2,3},{3,2},{4,5},{5,4},{6,7},{7,6},{8,9},{9,8},{10,11... | collective-permute-start | bytes 73736 | tf_op jit(solution)/shard_map/ppermute | solution.py:364
  44.1 6.5 %collective-permute-start.1 = (f32[4096]{0:T(1024)S(1)}, f32[4096]{0:T(1024)S(1)}, u32[]{:S(2)}, u32[]{:S(2)}) collective-permute-start(f32[4096]{0:T(1024)S(1)} %copy-done.6), channel_id=1, source_target_pairs={{1,2},{3,4},{5,6},{7,8},{9,10},{11,12},{13,14},{15,16},{17,18},{19... | collective-permute-start | bytes 49160 | tf_op jit(solution)/shard_map/ppermute | solution.py:364
  47.2 3.4 %copy-start.5 = (s32[16,3]{0,1:T(4,128)S(1)}, s32[16,3]{0,1:T(4,128)}, u32[]{:S(2)}) copy-start(s32[16,3]{0,1:T(4,128)} %param.8) | copy-start | bytes 580
  54.6 18.6 %all-to-all-start.1 = ((f32[64,1,128]{2,1,0:T(1,128)}), f32[64,1,128]{2,1,0:T(1,128)S(1)}, u32[]{:S(2)}, u32[]{:S(2)}) async-start(f32[64,1,128]{2,1,0:T(1,128)} %shard_map.87), calls=%async_computation.1 | async-start | bytes 65536 | tf_op jit(solution)/shard_map/all_to_all | solution.py:372
  63.4 10.0 %collective-permute-start.2 = (bf16[16,256]{1,0:T(8,128)(2,1)S(1)}, bf16[16,256]{1,0:T(8,128)(2,1)S(1)}, u32[]{:S(2)}, u32[]{:S(2)}) collective-permute-start(bf16[16,256]{1,0:T(8,128)(2,1)S(1)} %get-tuple-element.24.refs_1_.refs_0_.refs_2_), channel_id=1, source_target_pairs={{0,1},{1,0},{2,3},{3,2},{4,5},{5,4},{6,7},{7,6},{8,9},{9,8},{10,11... | collective-permute-start | bytes 24584 | tf_op jit(solution)/shard_map/ppermute | solution.py:364
  63.5 9.8 %collective-permute-start.3 = (bf16[16,256]{1,0:T(8,128)(2,1)S(1)}, bf16[16,256]{1,0:T(8,128)(2,1)S(1)}, u32[]{:S(2)}, u32[]{:S(2)}) collective-permute-start(bf16[16,256]{1,0:T(8,128)(2,1)S(1)} %get-tuple-element.24.refs_1_.refs_0_.refs_2_), channel_id=1, source_target_pairs={{1,2},{3,4},{5,6},{7,8},{9,10},{11,12},{13,14},{15,16},{17,18},{19... | collective-permute-start | bytes 24584 | tf_op jit(solution)/shard_map/ppermute | solution.py:364
  73.2 6.2 %collective-permute-start.4 = (f32[1,256]{1,0:T(1,128)S(1)}, f32[1,256]{1,0:T(1,128)S(1)}, u32[]{:S(2)}, u32[]{:S(2)}) collective-permute-start(f32[1,256]{1,0:T(1,128)S(1)} %shard_map.88.refs_9_.refs_2_), channel_id=1, source_target_pairs={{0,1},{1,0},{2,3},{3,2},{4,5},{5,4},{6,7},{7,6},{8,9},{9,8},{10,11... | collective-permute-start | bytes 3080 | tf_op jit(solution)/shard_map/ppermute | solution.py:364
  73.4 2.8 %copy-start = (bf16[16,3,256,256]{3,2,1,0:T(8,128)(2,1)S(1)}, bf16[16,3,256,256]{3,2,1,0:T(8,128)(2,1)}, u32[]{:S(2)}) copy-start(bf16[16,3,256,256]{3,2,1,0:T(8,128)(2,1)} %refs_5_.1) | copy-start | bytes 18874372
  76.2 1.8 %copy-start.3 = (bf16[11,32,4096]{2,1,0:T(8,128)(2,1)S(1)}, bf16[11,32,4096]{2,1,0:T(8,128)(2,1)}, u32[]{:S(2)}) copy-start(bf16[11,32,4096]{2,1,0:T(8,128)(2,1)} %param.9) | copy-start | bytes 8650756

commit v5 on v4

--- a/solution.py
+++ b/solution.py
@@ -12,6 +12,7 @@
 BF16 = jnp.bfloat16
 LANES = 128
 SUBLANES = 8
+VMEM_LIMIT = 67043328
 RING = 32
 NT = (((1,), (1,)), ((), ()))
 TN = (((0,), (0,)), ((), ()))
@@ -79,13 +80,44 @@
     sums[...] = sums_row(total)
 
 
-def project_early_kernel(sizes, *refs):
+def early_kernel(
+    sizes, slip_hbm, far_right, ranks_hbm, blocks_hbm, left_hbm, sums_hbm, own_hbm, partial_hbm,
+    sums, own, partial, slip, right_cross, sems, ranks, blocks, right, left,
+):
+    steps = sizes["steps"]
+
+    def put(values, target, number):
+        copy = pltpu.make_async_copy(values, target, sems.at[steps + number])
+        copy.start()
+        return copy
+
     @pl.when(early(RING // 2))
     def _():
+        project(sizes, slip_hbm, far_right, sums, own, slip, right_cross, sems)
+        for copy in (put(sums, sums_hbm, 1), put(own, own_hbm, 2)):
+            copy.wait()
+
+    @pl.when(ahead(sizes))
+    def _():
+        copies = (
+            put(far_right.at[pl.ds(0, right.shape[0])], right, 1),
+            put(left_hbm.at[pl.ds(0, left.shape[0])], left, 2),
+            put(blocks_hbm.at[:, pl.ds(0, 1)], blocks, 3),
+            put(ranks_hbm, ranks, 4),
+        )
+        for copy in copies:
+            copy.wait()
+        partial[...] = own_part(sizes, ranks, own, blocks, right, left)
+        put(partial, partial_hbm, 5).wait()
+
+
+def late_kernel(sizes, *refs):
+    @pl.when(jnp.logical_not(early(RING // 2)))
+    def _():
         project(sizes, *refs)
 
 
-def project_late_kernel(sizes, slip_hbm, far_right, early_sums, early_own, sums, own, *scratch):
+def choose_kernel(sizes, early_sums, early_own, late_sums, late_own, sums, own):
     done = early(RING // 2)
 
     @pl.when(done)
@@ -95,7 +127,8 @@
 
     @pl.when(jnp.logical_not(done))
     def _():
-        project(sizes, slip_hbm, far_right, sums, own, *scratch)
+        sums[...] = late_sums[...]
+        own[...] = late_own[...]
 
 
 def place_of(chip, chips):
@@ -190,25 +223,6 @@
     return [rows[k * leaves : (k + 1) * leaves, :] for k in range(near - 1)]
 
 
-def own_ahead_kernel(
-    sizes, ranks_hbm, own, blocks_hbm, right_hbm, left_hbm, partial, ranks, blocks, right, left, sems
-):
-    @pl.when(ahead(sizes))
-    def _():
-        local_rows = pl.ds(0, right.shape[0])
-        copies = [
-            pltpu.make_async_copy(right_hbm.at[local_rows], right, sems.at[0]),
-            pltpu.make_async_copy(left_hbm.at[local_rows], left, sems.at[1]),
-            pltpu.make_async_copy(blocks_hbm.at[:, pl.ds(0, 1)], blocks, sems.at[2]),
-            pltpu.make_async_copy(ranks_hbm, ranks, sems.at[3]),
-        ]
-        for copy in copies:
-            copy.start()
-        for copy in copies:
-            copy.wait()
-        partial[...] = own_part(sizes, ranks, own, blocks, right, left)
-
-
 def second_core():
     return lax.axis_index("leaf") % 2 == 1
 
@@ -348,15 +362,15 @@
     order = sorted(range(chips), key=lambda chip: place_of(chip, chips))
     groups = [[chip * 2 + core for chip in order] for core in range(2)]
 
-    def call(kernel, out_shape, specs, operands, mib=4, scratch=(), cost=None):
+    def call(kernel, out_shape, specs, operands, mib=4, scratch=(), cost=None, out_spec=VMEM_SPEC):
         outs = out_shape if isinstance(out_shape, tuple) else (out_shape,)
         return pl.pallas_call(
             lambda *refs: kernel(sizes, *refs),
             out_shape=out_shape,
             in_specs=specs,
-            out_specs=tuple(VMEM_SPEC for _ in outs) if isinstance(out_shape, tuple) else VMEM_SPEC,
+            out_specs=tuple(out_spec for _ in outs) if isinstance(out_shape, tuple) else out_spec,
             scratch_shapes=scratch,
-            compiler_params=pltpu.CompilerParams(vmem_limit_bytes=mib << 20),
+            compiler_params=pltpu.CompilerParams(vmem_limit_bytes=min(mib << 20, VMEM_LIMIT)),
             cost_estimate=cost,
         )(*operands)
 
@@ -385,26 +399,26 @@
         pltpu.VMEM((cross_rows, patches), BF16),
         pltpu.SemaphoreType.DMA((sizes["steps"] + 1,)),
     ]
-    sums, own = call(
-        project_early_kernel, (sums_shape, partial_shape), [ANY_SPEC] * 2, hbm(slip, right),
-        scratch=project_scratch,
-    )
-    before = call(
-        own_ahead_kernel, partial_shape, [ANY_SPEC, VMEM_SPEC] + [ANY_SPEC] * 3,
-        (*hbm(far_ranks), own, *hbm(near_blocks, right, left)), 8,
+    *from_early, before = call(
+        early_kernel, (sums_shape, partial_shape, partial_shape), [ANY_SPEC] * 5,
+        hbm(slip, right, far_ranks, near_blocks, left), 64,
         [
+            pltpu.VMEM(sums_shape.shape, F32),
+            pltpu.VMEM(partial_shape.shape, F32),
+            pltpu.VMEM(partial_shape.shape, F32),
+            *project_scratch[:-1],
+            pltpu.SemaphoreType.DMA((sizes["steps"] + 6,)),
             pltpu.VMEM(far_ranks.shape, jnp.int32),
             pltpu.VMEM((leaves, 1, leaf_size, leaf_size), BF16),
             pltpu.VMEM((local_rows, patches), BF16),
             pltpu.VMEM((local_rows, patches), BF16),
-            pltpu.SemaphoreType.DMA((4,)),
         ],
-    )
-    sums, own = call(
-        project_late_kernel, (sums_shape, partial_shape), [ANY_SPEC] * 2 + [VMEM_SPEC] * 2,
-        (*hbm(slip, right), sums, own),
-        scratch=project_scratch,
-    )
+        out_spec=ANY_SPEC,
+    )
+    from_late = call(
+        late_kernel, (sums_shape, partial_shape), [ANY_SPEC] * 2, hbm(slip, right), scratch=project_scratch
+    )
+    sums, own = call(choose_kernel, (sums_shape, partial_shape), [VMEM_SPEC] * 4, (*from_early, *from_late), 1)
     packet = exchange(sums, before, own)
     second, packet = call(
         own_second_kernel, (partial_shape, shape(packet.shape, F32)), [VMEM_SPEC] * 7,

time: 81.4 us -> 86.4 us (1.061)
  local copies, waits for them, and re-layouts: 5.16 us -> 9.92 us
  blocking collectives: 37.1 us -> 35.9 us
  Pallas kernels: 12 us -> 13.1 us
    unnamed x18 -> x34, local copies, waits for them, and re-layouts: 5.16 us -> 9.92 us
    all_to_all x1, blocking collectives: 37.1 us -> 35.9 us  [exchange(): lax.all_to_all(outgoing, 'leaf', 0, 0, axis_index_groups=groups, tiled=True)]
    pallas_call x14, Pallas kernels: 12 us -> 13.1 us  [call(): pl.pallas_call(lambda *refs: kernel(sizes, *refs), out_shape=out_shape, i...]
where the time goes in v5:
time: 86.4 us; the launch traced here: 85.1 us
  blocking collectives  35.9 us (42%)
  Pallas kernels  13.1 us (15%)
  starting transfers between devices  13 us (15%)
  waiting for transfers between devices  12.2 us (14%)
  local copies, waits for them, and re-layouts  9.92 us (11%)
  between operations  0.93 us (1%)
    all_to_all x1, blocking collectives, exchange(): lax.all_to_all(outgoing, 'leaf', 0, 0, axis_index_groups=groups, tiled=True)  35.9 us
    pallas_call x14, Pallas kernels, call(): pl.pallas_call(lambda *refs: kernel(sizes, *refs), out_shape=out_shape, i...  13.1 us
    unnamed x34, local copies, waits for them, and re-layouts  9.92 us
    all_to_all x1, waiting for transfers between devices, exchange(): lax.all_to_all(outgoing, 'leaf', 0, 0, axis_index_groups=groups, tiled=True)  8.96 us
    all_to_all x1, starting transfers between devices, exchange(): lax.all_to_all(outgoing, 'leaf', 0, 0, axis_index_groups=groups, tiled=True)  8.81 us
    ppermute x5, starting transfers between devices, permute(): return lax.ppermute(array, 'leaf', pairs)  4.22 us
    ppermute x5, waiting for transfers between devices, permute(): return lax.ppermute(array, 'leaf', pairs)  3.26 us
  transfers between devices with their start and end apart: 6, of which 2 were waited for; matrix products, arithmetic and copies ran while one was open for 0% of the time, Pallas kernels for 2%

profile of v5, /device:TPU:40, one launch (start us, length us, event | category | flops | bytes accessed | tf_op | source)
XLA Modules:
  0.0 85.1 jit_solution(17486709536201568313)
XLA Ops:
  0.7 0.6 copy-done.7
  1.3 0.6 copy-done.11
  1.9 6.5 %shard_map.77 = (f32[1,256]{1,0:T(1,128)}, f32[16,256]{1,0:T(8,128)}, f32[16,256]{1,0:T(8,128)}) custom-call(f32[32,128]{1,0:T(8,128)} %bitcast.27, bf16[352,4096]{1,0:T(8,128)(2,1)} %bitcast.10, s32[16,11]{1,0:T(8,128)} %refs_1_.1, bf16[16,3,256,256]{3,2,1,0:T(8,128)(2,1)} %refs_5_.1, bf16[352,4096]{1,0:T(8,128)(2,1)} %bitcast.16), custom_call_target="tpu_custom_call" | custom-call | tf_op jit(solution)/shard_map/pallas_call | solution.py:367
  8.4 0.7 copy-done.8
  9.1 0.7 copy-done.9
  9.8 0.7 copy-done.12
  10.5 0.6 copy-done.13
  11.1 0.9 %copy-done.5 = f32[16,256]{1,0:T(8,128)S(1)} copy-done((f32[16,256]{1,0:T(8,128)S(1)}, f32[16,256]{1,0:T(8,128)}, u32[]{:S(2)}) %copy-start.5) | copy-done | bytes 16408
  12.1 35.9 %all_to_all.10.refs_1_ = f32[64,1,128]{2,1,0:T(1,128)S(1)} all-to-all(f32[64,1,128]{2,1,0:T(1,128)S(1)} %shard_map.80), channel_id=1, replica_groups={{94,92,90,88,86,84,82,80,78,76,74,72,70,68,66,64,62,60,58,56,54,52,50,4..., dimensions={0} | all-to-all | bytes 65536 | tf_op jit(solution)/shard_map/all_to_all | solution.py:386
  48.1 0.1 collective-permute-start
  48.3 0.5 copy-done.14
  48.8 3.1 %collective-permute-start.1 = (f32[4096]{0:T(1024)S(1)}, f32[4096]{0:T(1024)S(1)}, u32[]{:S(2)}, u32[]{:S(2)}) collective-permute-start(f32[4096]{0:T(1024)S(1)} %copy-done.14), channel_id=1, source_target_pairs={{1,2},{3,4},{5,6},{7,8},{9,10},{11,12},{13,14},{15,16},{17,18},{19... | collective-permute-start | bytes 49160 | tf_op jit(solution)/shard_map/ppermute | solution.py:378
  52.0 3.3 %collective-permute-done.1 = f32[4096]{0:T(1024)S(1)} collective-permute-done((f32[4096]{0:T(1024)S(1)}, f32[4096]{0:T(1024)S(1)}, u32[]{:S(2)}, u32[]{:S(2)}) %collective-permute-start.1) | collective-permute-done | bytes 16416 | tf_op jit(solution)/shard_map/ppermute | solution.py:378
  55.3 1.5 %shard_map.84 = (f32[32,128]{1,0:T(8,128)S(1)}, bf16[16,256]{1,0:T(8,128)(2,1)S(1)}) custom-call(s32[3,16]{1,0:T(4,128)S(1)} %bitcast.24, f32[16,256]{1,0:T(8,128)S(1)} %get-tuple-element.28.refs_1_, f32[16,224]{1,0:T(8,128)S(1)} %get-tuple-element.29.refs_2_.refs_1_, f32[16,256]{1,0:T(8,128)S(1)} %get-tuple-element.23.refs_2_.refs_1_.refs_3_.refs_9_, ...), custom_call_target="tpu_custom_call" | custom-call | tf_op jit(solution)/shard_map/pallas_call | solution.py:367
  56.8 1.7 %shard_map.85 = (f32[16,256]{1,0:T(8,128)S(1)}, f32[1,256]{1,0:T(1,128)S(1)}) custom-call(s32[16,11]{1,0:T(8,128)S(1)} %copy-done.4, bf16[16,256]{1,0:T(8,128)(2,1)S(1)} %get-tuple-element.30.refs_1_.refs_0_.refs_2_, bf16[16,3,256,256]{3,2,1,0:T(8,128)(2,1)S(1)} %bitcast.8, bf16[352,4096]{1,0:T(8,128)(2,1)S(1)} %bitcast.13, bf16[352,4096]{1,0:T(8,128)(2,1)S(1)} %bitcast.20), custom_call_target="tpu_custom_call" | custom-call | tf_op jit(solution)/shard_map/pallas_call | solution.py:367
  58.6 0.7 shard_map.87
  59.3 8.8 %all-to-all-start.1 = ((f32[64,1,128]{2,1,0:T(1,128)}), f32[64,1,128]{2,1,0:T(1,128)S(1)}, u32[]{:S(2)}, u32[]{:S(2)}) async-start(f32[64,1,128]{2,1,0:T(1,128)} %shard_map.87), calls=%async_computation.1 | async-start | bytes 65536 | tf_op jit(solution)/shard_map/all_to_all | solution.py:386
  68.1 0.1 collective-permute-start.2
  68.2 0.7 collective-permute-start.3
  68.9 9.0 %all-to-all-done.1.refs_1_ = f32[64,1,128]{2,1,0:T(1,128)S(1)} async-done(((f32[64,1,128]{2,1,0:T(1,128)}), f32[64,1,128]{2,1,0:T(1,128)S(1)}, u32[]{:S(2)}, u32[]{:S(2)}) %all-to-all-start.1) | async-done | bytes 32800 | tf_op jit(solution)/shard_map/all_to_all | solution.py:386
  78.1 2.8 %copy-done = bf16[16,3,256,256]{3,2,1,0:T(8,128)(2,1)S(1)} copy-done((bf16[16,3,256,256]{3,2,1,0:T(8,128)(2,1)S(1)}, bf16[16,3,256,256]{3,2,1,0:T(8,128)(2,1)}, u32[]{:S(2)}) %copy-start) | copy-done | bytes 6291480
  80.9 1.8 %copy-done.3 = bf16[11,32,4096]{2,1,0:T(8,128)(2,1)S(1)} copy-done((bf16[11,32,4096]{2,1,0:T(8,128)(2,1)S(1)}, bf16[11,32,4096]{2,1,0:T(8,128)(2,1)}, u32[]{:S(2)}) %copy-start.3) | copy-done | bytes 2883608
  82.7 1.4 %shard_map.89.refs_0_ = f32[16,256]{1,0:T(8,128)S(1)} custom-call(s32[3,16]{1,0:T(4,128)S(1)} %bitcast.25, s32[16,11]{1,0:T(8,128)S(1)} %copy-done.4, bf16[16,256]{1,0:T(8,128)(2,1)S(1)} %get-tuple-element.30.refs_1_.refs_0_.refs_2_, bf16[16,256]{1,0:T(8,128)(2,1)S(1)} %collective-permute-done.2.refs_3_, bf16[16,256]{1,0:T(8,128)(2,1)S(1)} %collective-permute-done.3.refs_4_, ...), custom_call_target="tpu_custom_call" | custom-call | tf_op jit(solution)/shard_map/pallas_call | solution.py:367
  84.1 1.0 %shard_map.90 = (f32[32,128]{1,0:T(8,128)}, f32[32,128]{1,0:T(8,128)}) custom-call(f32[16,256]{1,0:T(8,128)S(1)} %shard_map.89.refs_0_, f32[16,224]{1,0:T(8,128)S(1)} %get-tuple-element.29.refs_2_.refs_1_, f32[1,256]{1,0:T(1,128)S(1)} %shard_map.88.refs_9_.refs_2_, f32[1,256]{1,0:T(1,128)S(1)} %collective-permute-done.4.refs_3_, ...), custom_call_target="tpu_custom_call" | custom-call | tf_op jit(solution)/shard_map/pallas_call | solution.py:367
  (38 shorter events, 0.6 us)
Async XLA Ops:
  0.7 0.6 copy-start.7
  1.3 0.6 copy-start.11
  8.4 0.7 copy-start.8
  9.1 0.7 copy-start.9
  9.8 0.7 copy-start.12
  10.5 0.6 copy-start.13
  11.1 36.9 %slice-start = ((s8[6291456]{0:T(1024)(128)(4,1)}), s8[4194304]{0:T(1024)(128)(4,1)S(1)}, s32[]{:S(2)}) async-start(s8[6291456]{0:T(1024)(128)(4,1)} %bitcast.7), calls=%async_computation.2 | async-start | bytes 8388608
  11.1 0.9 %copy-start.5 = (f32[16,256]{1,0:T(8,128)S(1)}, f32[16,256]{1,0:T(8,128)}, u32[]{:S(2)}) copy-start(f32[16,256]{1,0:T(8,128)} %get-tuple-element.24.refs_1_.refs_5_) | copy-start | bytes 49156
  12.0 36.0 %slice-start.1 = ((s8[6291456]{0:T(1024)(128)(4,1)}), s8[2097152]{0:T(1024)(128)(4,1)S(1)}, s32[]{:S(2)}) async-start(s8[6291456]{0:T(1024)(128)(4,1)} %bitcast.7), calls=%async_computation.3 | async-start | bytes 4194304
  12.0 36.0 %copy-start.1 = (bf16[11,32,4096]{2,1,0:T(8,128)(2,1)S(1)}, bf16[11,32,4096]{2,1,0:T(8,128)(2,1)}, u32[]{:S(2)}) copy-start(bf16[11,32,4096]{2,1,0:T(8,128)(2,1)} %param.10) | copy-start | bytes 8650756
  12.0 36.0 %copy-start.2 = (bf16[11,32,4096]{2,1,0:T(8,128)(2,1)S(1)}, bf16[11,32,4096]{2,1,0:T(8,128)(2,1)}, u32[]{:S(2)}) copy-start(bf16[11,32,4096]{2,1,0:T(8,128)(2,1)} %param.9) | copy-start | bytes 8650756
  12.0 36.0 %copy-start.4 = (s32[16,11]{1,0:T(8,128)S(1)}, s32[16,11]{1,0:T(8,128)}, u32[]{:S(2)}) copy-start(s32[16,11]{1,0:T(8,128)} %refs_1_.1) | copy-start | bytes 2116
  12.0 36.1 %copy-start.6 = (f32[16,256]{1,0:T(8,128)S(1)}, f32[16,256]{1,0:T(8,128)}, u32[]{:S(2)}) copy-start(f32[16,256]{1,0:T(8,128)} %get-tuple-element.24.refs_1_.refs_5_) | copy-start | bytes 49156
  48.1 0.7 copy-start.14
  48.1 7.2 %collective-permute-start = (f32[24,256]{1,0:T(8,128)S(1)}, f32[24,256]{1,0:T(8,128)S(1)}, u32[]{:S(2)}, u32[]{:S(2)}) collective-permute-start(f32[24,256]{1,0:T(8,128)S(1)} %get-tuple-element.27.refs_7_.refs_4_), channel_id=1, source_target_pairs={{0,1},{1,0},{2,3},{3,2},{4,5},{5,4},{6,7},{7,6},{8,9},{9,8},{10,11... | collective-permute-start | bytes 73736 | tf_op jit(solution)/shard_map/ppermute | solution.py:378
  48.8 6.5 %collective-permute-start.1 = (f32[4096]{0:T(1024)S(1)}, f32[4096]{0:T(1024)S(1)}, u32[]{:S(2)}, u32[]{:S(2)}) collective-permute-start(f32[4096]{0:T(1024)S(1)} %copy-done.14), channel_id=1, source_target_pairs={{1,2},{3,4},{5,6},{7,8},{9,10},{11,12},{13,14},{15,16},{17,18},{19... | collective-permute-start | bytes 49160 | tf_op jit(solution)/shard_map/ppermute | solution.py:378
  51.9 3.4 %copy-start.10 = (s32[16,3]{0,1:T(4,128)S(1)}, s32[16,3]{0,1:T(4,128)}, u32[]{:S(2)}) copy-start(s32[16,3]{0,1:T(4,128)} %param.8) | copy-start | bytes 580
  59.3 18.6 %all-to-all-start.1 = ((f32[64,1,128]{2,1,0:T(1,128)}), f32[64,1,128]{2,1,0:T(1,128)S(1)}, u32[]{:S(2)}, u32[]{:S(2)}) async-start(f32[64,1,128]{2,1,0:T(1,128)} %shard_map.87), calls=%async_computation.1 | async-start | bytes 65536 | tf_op jit(solution)/shard_map/all_to_all | solution.py:386
  68.1 10.0 %collective-permute-start.2 = (bf16[16,256]{1,0:T(8,128)(2,1)S(1)}, bf16[16,256]{1,0:T(8,128)(2,1)S(1)}, u32[]{:S(2)}, u32[]{:S(2)}) collective-permute-start(bf16[16,256]{1,0:T(8,128)(2,1)S(1)} %get-tuple-element.30.refs_1_.refs_0_.refs_2_), channel_id=1, source_target_pairs={{0,1},{1,0},{2,3},{3,2},{4,5},{5,4},{6,7},{7,6},{8,9},{9,8},{10,11... | collective-permute-start | bytes 24584 | tf_op jit(solution)/shard_map/ppermute | solution.py:378
  68.2 9.8 %collective-permute-start.3 = (bf16[16,256]{1,0:T(8,128)(2,1)S(1)}, bf16[16,256]{1,0:T(8,128)(2,1)S(1)}, u32[]{:S(2)}, u32[]{:S(2)}) collective-permute-start(bf16[16,256]{1,0:T(8,128)(2,1)S(1)} %get-tuple-element.30.refs_1_.refs_0_.refs_2_), channel_id=1, source_target_pairs={{1,2},{3,4},{5,6},{7,8},{9,10},{11,12},{13,14},{15,16},{17,18},{19... | collective-permute-start | bytes 24584 | tf_op jit(solution)/shard_map/ppermute | solution.py:378
  77.9 6.2 %collective-permute-start.4 = (f32[1,256]{1,0:T(1,128)S(1)}, f32[1,256]{1,0:T(1,128)S(1)}, u32[]{:S(2)}, u32[]{:S(2)}) collective-permute-start(f32[1,256]{1,0:T(1,128)S(1)} %shard_map.88.refs_9_.refs_2_), channel_id=1, source_target_pairs={{0,1},{1,0},{2,3},{3,2},{4,5},{5,4},{6,7},{7,6},{8,9},{9,8},{10,11... | collective-permute-start | bytes 3080 | tf_op jit(solution)/shard_map/ppermute | solution.py:378
  78.1 2.8 %copy-start = (bf16[16,3,256,256]{3,2,1,0:T(8,128)(2,1)S(1)}, bf16[16,3,256,256]{3,2,1,0:T(8,128)(2,1)}, u32[]{:S(2)}) copy-start(bf16[16,3,256,256]{3,2,1,0:T(8,128)(2,1)} %refs_5_.1) | copy-start | bytes 18874372
  80.9 1.8 %copy-start.3 = (bf16[11,32,4096]{2,1,0:T(8,128)(2,1)S(1)}, bf16[11,32,4096]{2,1,0:T(8,128)(2,1)}, u32[]{:S(2)}) copy-start(bf16[11,32,4096]{2,1,0:T(8,128)(2,1)} %param.9) | copy-start | bytes 8650756
